TPU v7x, 32 devices: a whole 2x2x4 slice. The times are simulated.
32 devices in a mesh: gx: 8 (over z, x), col: 4 (over y, core).
Axes of the slice: x: 2, y: 2, z: 4, core: 2. Of those that a mesh axis runs over, the one named last changes fastest.
Arguments:
- grid_field: bfloat16 [64, 32, 256, 128], P('col', 'gx'), may hold values from -6 to 6
- tucker_core: float32 [2, 32, 32, 8, 8, 4], P(None, 'col'), may hold values from -0.5 to 0.5
- in_factor: float32 [64, 32], P('col'), may hold values from -0.75 to 0.75
- out_factor: float32 [64, 32], P('col'), may hold values from -1 to 1
- x_factor: float32 [32, 8], replicated, may hold values from -4 to 4
- y_factor: float32 [32, 8], replicated, may hold values from -4 to 4
- z_factor: float32 [16, 4], replicated, may hold values from -4 to 4
- kx_reach: int32 [32, 16], replicated, may hold values from 1 to 17
Outputs:
- spectral_out: bfloat16 [64, 32, 256, 128], P('col', 'gx')
All inputs are finite; a program needn't handle non-finite values.
Results may differ from a plain program's by a relative error of at most 0.001.
Values sent between devices are 32-bit elements; how exact they have to be, the bound alone decides.
A program may use at most 64 MiB of HBM per device.

v0:
```python
import functools
import math

import jax
import jax.numpy as jnp
import numpy as np
from jax import lax
from jax.experimental import pallas as pl
from jax.experimental.pallas import tpu as pltpu
from jax.sharding import PartitionSpec as P

MESH = pl.DeviceIdType.MESH
VMEM = pl.BlockSpec(memory_space=pltpu.VMEM)
F32 = jnp.float32
BF16 = jnp.bfloat16


def slot_freq(slot_count):
    slot_index = jnp.arange(slot_count, dtype=jnp.int32)
    return jnp.where(slot_index < slot_count // 2, slot_index, slot_index - slot_count)


def phase_table(positions, extent, slot_count, direction):
    phase_steps = positions[:, None] * slot_freq(slot_count)[None, :] % extent
    radians = 2.0 * math.pi / extent * phase_steps.astype(jnp.float32)
    norm_scale = 1.0 / math.sqrt(extent)
    cosine = jnp.cos(radians) * norm_scale
    sine_part = direction * jnp.sin(radians) * norm_scale
    return jnp.stack([jnp.stack([cosine, -sine_part], 1), jnp.stack([sine_part, cosine], 1)], 1)


def z_tables(grid_z, modes_z):
    z_index = jnp.arange(grid_z, dtype=jnp.int32)
    kz_index = jnp.arange(modes_z, dtype=jnp.int32)
    phase_steps = z_index[:, None] * kz_index[None, :] % grid_z
    radians = 2.0 * math.pi / grid_z * phase_steps.astype(jnp.float32)
    norm_scale = 1.0 / math.sqrt(grid_z)
    cosine = jnp.cos(radians) * norm_scale
    sine_part = jnp.sin(radians) * norm_scale
    forward = jnp.stack([cosine, -sine_part], 1)
    weight = jnp.where(kz_index == 0, 1.0, 2.0).astype(jnp.float32)
    backward = jnp.stack([(cosine * weight[None, :]).T, -(sine_part * weight[None, :]).T], 0)
    return (forward, backward)


def plain_device(
    grid_field, tucker_core, in_factor, out_factor, x_factor, y_factor, z_factor, kx_reach
):
    highest = lax.Precision.HIGHEST
    channels, planes, grid_y, grid_z = grid_field.shape
    modes_x = x_factor.shape[0]
    modes_y = y_factor.shape[0]
    modes_z = z_factor.shape[0]
    width_gx = lax.axis_size("gx")
    grid_x = planes * width_gx
    columns = modes_y * modes_z
    col_dev = columns // width_gx
    slab_index = lax.axis_index("gx")
    z_forward, z_backward = z_tables(grid_z, modes_z)
    y_forward = phase_table(jnp.arange(grid_y, dtype=jnp.int32), grid_y, modes_y, 1.0)
    x_forward = phase_table(jnp.arange(grid_x, dtype=jnp.int32), grid_x, modes_x, 1.0)
    values = grid_field.astype(jnp.float32)
    z_spectrum = jnp.einsum("cxyz,zpl->cxply", values, z_forward, precision=highest)
    y_spectrum = jnp.einsum("cxply,ypqj->qcxjl", z_spectrum, y_forward, precision=highest)
    y_spectrum = y_spectrum.reshape(2, channels, planes, columns)
    first_col = slab_index * col_dev
    reach_dev = lax.dynamic_slice_in_dim(kx_reach.reshape(-1), first_col, col_dev)
    kept_mask = (jnp.abs(slot_freq(modes_x))[:, None] < reach_dev[None, :]).astype(jnp.float32)
    arrived = lax.all_to_all(y_spectrum, "gx", split_axis=3, concat_axis=2, tiled=True)
    spectrum = jnp.einsum("pcxm,xpqk->qckm", arrived, x_forward, precision=highest)
    partial_value = jnp.einsum("qckm,cr->qrkm", spectrum, in_factor, precision=highest)
    amplitude = lax.psum_scatter(partial_value, "col", scatter_dimension=1, tiled=True)
    amplitude = amplitude * kept_mask[None, None]
    column = first_col + jnp.arange(col_dev, dtype=jnp.int32)
    pick_y = (column[:, None] // modes_z == jnp.arange(modes_y, dtype=jnp.int32)[None, :]).astype(
        jnp.float32
    )
    pick_z = (column[:, None] % modes_z == jnp.arange(modes_z, dtype=jnp.int32)[None, :]).astype(
        jnp.float32
    )
    y_rows = jnp.dot(pick_y, y_factor, precision=highest)
    z_rows = jnp.dot(pick_z, z_factor, precision=highest)
    core_cols = jnp.einsum("prsabe,mb,me->prsam", tucker_core, y_rows, z_rows, precision=highest)
    kernel = jnp.einsum("prsam,ka->prskm", core_cols, x_factor, precision=highest)
    mixed_re = jnp.einsum("rskm,rkm->skm", kernel[0], amplitude[0], precision=highest) - jnp.einsum(
        "rskm,rkm->skm", kernel[1], amplitude[1], precision=highest
    )
    mixed_im = jnp.einsum("rskm,rkm->skm", kernel[0], amplitude[1], precision=highest) + jnp.einsum(
        "rskm,rkm->skm", kernel[1], amplitude[0], precision=highest
    )
    mixed_sum = lax.psum(jnp.stack([mixed_re, mixed_im]), "col")
    out_spec = jnp.einsum("os,qskm->qokm", out_factor, mixed_sum, precision=highest)
    x_backward = phase_table(jnp.arange(grid_x, dtype=jnp.int32), grid_x, modes_x, -1.0)
    x_values = jnp.einsum("pckm,xpqk->qcxm", out_spec, x_backward, precision=highest)
    returned = lax.all_to_all(x_values, "gx", split_axis=2, concat_axis=3, tiled=True)
    returned = returned.reshape(2, channels, planes, modes_y, modes_z)
    y_backward = phase_table(jnp.arange(grid_y, dtype=jnp.int32), grid_y, modes_y, -1.0)
    y_values = jnp.einsum("pcxjl,ypqj->cxqly", returned, y_backward, precision=highest)
    result = jnp.einsum("cxqly,qlz->cxyz", y_values, z_backward, precision=highest)
    return result.astype(jnp.bfloat16)


def split_np(table):
    high = table.astype(np.float32).astype(BF16)
    low = (table - high.astype(np.float64)).astype(np.float32).astype(BF16)
    return high, low


def split(values):
    high = values.astype(BF16)
    return high, (values - high.astype(F32)).astype(BF16)


def freqs(slots):
    index = np.arange(slots)
    return np.where(index < slots // 2, index, index - slots)


def waves(extent, frequencies):
    steps = np.arange(extent)[:, None] * frequencies[None, :] % extent
    angle = 2.0 * np.pi / extent * steps
    return np.cos(angle) / math.sqrt(extent), np.sin(angle) / math.sqrt(extent)


def dot(a, b):
    return jnp.dot(a, b, preferred_element_type=F32)


def forward_tables(grid_y, grid_z, modes_y, modes_z, planes):
    cos_y, sin_y = waves(grid_y, freqs(modes_y))
    high, low = split_np(np.concatenate([cos_y.T, -sin_y.T], 0))
    y_table = np.concatenate([high, low], 0)
    cos_z, sin_z = waves(grid_z, np.arange(modes_z))
    table = np.zeros((planes, 2, grid_z, modes_z, planes, 2))
    for plane in range(planes):
        table[plane, 0, :, :, plane, 0] = cos_z
        table[plane, 0, :, :, plane, 1] = -sin_z
        table[plane, 1, :, :, plane, 0] = sin_z
        table[plane, 1, :, :, plane, 1] = cos_z
    high, low = split_np(table.reshape(planes * 2 * grid_z, -1))
    return y_table, np.concatenate([high, low], 1)


def inverse_tables(grid_y, grid_z, modes_y, modes_z, planes):
    cos_y, sin_y = waves(grid_y, freqs(modes_y))
    high, low = split_np(np.concatenate([cos_y, -sin_y], 1))
    y_table = np.concatenate([high, high, low], 1)
    cos_z, sin_z = waves(grid_z, np.arange(modes_z))
    weight = np.where(np.arange(modes_z) == 0, 1.0, 2.0)
    cos_z, sin_z = (cos_z * weight).T, (sin_z * weight).T
    table = np.zeros((modes_z, planes, 2, planes, 2, grid_z))
    for plane in range(planes):
        table[:, plane, 0, plane, 0, :] = cos_z
        table[:, plane, 1, plane, 0, :] = -sin_z
        table[:, plane, 0, plane, 1, :] = sin_z
        table[:, plane, 1, plane, 1, :] = cos_z
    high, low = split_np(table.reshape(modes_z * planes * 2, -1))
    return y_table, high, low


def x_tables(grid_x, modes_x):
    cos_x, sin_x = waves(grid_x, freqs(modes_x))
    real = np.stack([cos_x.T, sin_x.T], 2).reshape(modes_x, -1)
    imag = np.stack([-sin_x.T, cos_x.T], 2).reshape(modes_x, -1)
    high, low = split_np(np.concatenate([real, imag, -imag, real], 0))
    forward = np.concatenate([high, high, low], 1)
    real = np.concatenate([cos_x, -sin_x], 1)
    imag = np.concatenate([sin_x, cos_x], 1)
    high, low = split_np(np.stack([real, imag], 1).reshape(grid_x * 2, -1))
    backward = np.concatenate([high, high, low], 1)
    return forward, backward


def selectors(width_col, rank_x, rank_dev, rank_z, rank_out):
    wide = np.arange(width_col * rank_x * rank_dev)
    rank_in = wide // (rank_x * rank_dev) * rank_dev + wide % rank_dev
    x_pick = wide // rank_dev % rank_x == np.arange(rank_x)[:, None]
    in_pick = rank_in == np.arange(width_col * rank_dev)[:, None]
    slim = np.arange(rank_z * rank_out)
    z_pick = slim // rank_out == np.arange(rank_z)[:, None]
    out_pick = slim % rank_out == np.arange(rank_out)[:, None]
    return [pick.astype(np.float32) for pick in (x_pick, in_pick, z_pick, out_pick)]


def spread(values, pick, dim):
    return lax.dot_general(
        values, pick, (((dim,), (0,)), ((), ())), precision=lax.Precision.HIGHEST,
        preferred_element_type=F32,
    )


def fused_kernel(
    width_gx, width_col, field_ref, core_ref, in_ref, out_factor_ref, x_ref, z_ref, reach_ref,
    x_pick_ref, in_pick_ref, z_pick_ref, out_pick_ref, y_table_ref, z_table_ref, fore_ref, back_ref,
    out_ref, field, y_high, y_low, spec, arrived, cores, factor, factors, rank_ref, high_ref,
    low_ref, plane_ref, result_ref, field_sems, sends, recvs, core_sends, core_recvs, factor_sends,
    factor_recvs, back_sends, back_recvs, own,
):
    count = width_gx * width_col
    my_gx, my_col = lax.axis_index("gx"), lax.axis_index("col")
    me = my_gx * width_col + my_col
    channels, planes, _, grid_z = field.shape
    groups, modes_y, group, lanes = spec.shape
    modes_x, modes_z = x_ref.shape[1], z_ref.shape[1]
    barrier = pltpu.get_barrier_semaphore()

    def fetch(channel):
        return pltpu.make_async_copy(
            field_ref.at[channel], field.at[channel], field_sems.at[channel]
        )

    def begin(channel, carry):
        fetch(channel).start()
        return carry

    lax.fori_loop(0, channels, begin, 0)

    def place(peer):
        return peer // width_col, lax.rem(peer, width_col)

    def greet(step, carry):
        peer = lax.rem(me + step, count)
        pl.semaphore_signal(barrier, inc=1, device_id=place(peer), device_id_type=MESH)
        return carry

    lax.fori_loop(1, count, greet, 0)

    def remote(source, target, send_sem, recv_sem, device):
        return pltpu.make_async_remote_copy(
            src_ref=source, dst_ref=target, send_sem=send_sem, recv_sem=recv_sem,
            device_id=device, device_id_type=MESH,
        )

    in_wide = spread(in_ref[...], in_pick_ref[...], 1)
    factor[:channels] = in_wide[:, :lanes]
    factor[channels : 2 * channels] = in_wide[:, lanes:]
    factor[2 * channels :] = spread(out_factor_ref[...], out_pick_ref[...], 1)

    def spectrum_copy(part, peer, writer, device):
        return remote(
            spec.at[part, peer], arrived.at[part, writer], sends.at[part, peer],
            recvs.at[part, writer], device,
        )

    def core_copy(peer, writer, device):
        return remote(
            core_ref.at[peer], cores.at[writer], core_sends.at[peer], core_recvs.at[writer], device
        )

    def factor_copy(peer, writer, device):
        return remote(
            factor, factors.at[writer], factor_sends.at[peer], factor_recvs.at[writer], device
        )

    half = 2 * modes_y
    pair = 2
    for part in range(groups):

        def transform(step, carry, part=part):
            for offset in range(pair):
                local = step * pair + offset
                channel = part * group + local
                fetch(channel).wait()
                parts = []
                for plane in range(planes):
                    both = dot(y_table_ref[...], field[channel, plane])
                    y_values = both[:half] + both[half:]
                    parts += [y_values[:modes_y], y_values[modes_y:]]
                high, low = split(jnp.concatenate(parts, 1))
                rows = pl.ds(pl.multiple_of(local * modes_y, modes_y), modes_y)
                y_high[rows] = high
                y_low[rows] = low
            return carry

        lax.fori_loop(0, group // pair, transform, 0)
        both = dot(y_high[...], z_table_ref[...])
        value = both[:, :lanes] + both[:, lanes:] + dot(y_low[...], z_table_ref[:, :lanes])
        spec[part] = jnp.swapaxes(value.reshape(group, modes_y, lanes), 0, 1)
        if part == 0:
            pl.semaphore_wait(barrier, count - 1)
            for step in range(1, width_col):
                peer = lax.rem(my_col + step, width_col)
                factor_copy(peer, my_col, (my_gx, peer)).start()
                core_copy(peer, my_col, (my_gx, peer)).start()
            pltpu.make_async_copy(core_ref.at[my_col], cores.at[my_col], own.at[0]).start()
            pltpu.make_async_copy(factor, factors.at[my_col], own.at[1]).start()
        pltpu.make_async_copy(spec.at[part, me], arrived.at[part, me], own.at[3 + part]).start()

        def send(step, carry, part=part):
            peer = lax.rem(me + step, count)
            spectrum_copy(part, peer, me, place(peer)).start()
            return carry

        lax.fori_loop(1, count, send, 0)

    x_wide = spread(x_ref[...], x_pick_ref[...], 0)
    x_rows = jnp.concatenate([x_wide] * 4, 0)
    z_rows = spread(z_ref[...], z_pick_ref[...], 0)
    spot = lax.broadcasted_iota(jnp.int32, reach_ref.shape, 1)
    reach = jnp.where(spot == me, reach_ref[...].astype(F32), 0.0)
    reach = jnp.sum(reach, axis=1, keepdims=True)
    slot = lax.broadcasted_iota(jnp.int32, (modes_x, x_rows.shape[1]), 0)
    slot = jnp.where(slot < modes_x // 2, slot, modes_x - slot).astype(F32)
    slot = jnp.concatenate([slot] * 4, 0)

    for step in range(1, width_col):
        source = lax.rem(my_col + step, width_col)
        factor_copy(source, source, (my_gx, my_col)).wait_recv()
        core_copy(source, source, (my_gx, my_col)).wait_recv()
    pltpu.make_async_copy(core_ref.at[my_col], cores.at[my_col], own.at[0]).wait()
    pltpu.make_async_copy(factor, factors.at[my_col], own.at[1]).wait()

    lead = lanes // modes_z
    both_modes = 2 * modes_x
    ranks = x_rows.shape[1]
    core_rows = ranks // width_col

    def stacked_rows(ref, first, rows):
        return ref[:, first : first + rows, :].reshape(width_col * rows, lanes)

    in_rows = jnp.concatenate(
        [stacked_rows(factors, 0, channels), stacked_rows(factors, channels, channels)], 1
    )
    out_rows = stacked_rows(factors, 2 * channels, channels)
    in_high, in_low = split(in_rows)
    in_stack = jnp.concatenate([in_high, in_low, in_high], 0)
    core = jnp.concatenate(
        [stacked_rows(cores, 0, core_rows), stacked_rows(cores, core_rows, core_rows)], 0
    )
    core_high, core_low = split(core)
    core_both = jnp.concatenate([core_high, core_low], 1)
    out_high, out_low = split(out_rows)
    out_stack = jnp.concatenate([out_high, out_low], 0)

    for part in range(groups):
        pltpu.make_async_copy(spec.at[part, me], arrived.at[part, me], own.at[3 + part]).wait()

        def receive(step, carry, part=part):
            source = lax.rem(me + count - step, count)
            spectrum_copy(part, source, source, (my_gx, my_col)).wait_recv()
            return carry

        lax.fori_loop(1, count, receive, 0)

    for slab in range(width_gx):
        blocks = [
            arrived[part, slab * width_col + source]
            for source in range(width_col)
            for part in range(groups)
        ]
        block = jnp.concatenate(blocks, 0)
        high = block.astype(BF16).astype(F32)
        stacked = jnp.concatenate([high, high, block - high], 0)
        value = dot(stacked.T.astype(BF16), in_stack)
        rank_ref[:, slab * lead : (slab + 1) * lead, :] = value.reshape(modes_z, lead, ranks)
    for l in range(modes_z):
        high, low = split(rank_ref[l])
        value = dot(fore_ref[...], jnp.concatenate([high, low, high], 0))
        value = value * jnp.where(slot < reach[l : l + 1], x_rows, 0.0)
        value = jnp.concatenate([value[:both_modes], value[both_modes:]], 1)
        rows = slice(l * both_modes, (l + 1) * both_modes)
        high_ref[rows], low_ref[rows] = split(value)
    both = dot(high_ref[...], core_both)
    mixed = both[:, :lanes] + both[:, lanes:] + dot(low_ref[...], core_high)
    for l in range(modes_z):
        value = mixed[l * both_modes : (l + 1) * both_modes] * z_rows[l : l + 1]
        high, low = split(value)
        value = dot(back_ref[...], jnp.concatenate([high, low, high], 0))
        plane_ref[:, l] = value.reshape(width_gx, lead, lanes)

    def back_copy(peer, writer, device):
        return remote(
            result_ref.at[peer], out_ref.at[writer], back_sends.at[peer], back_recvs.at[writer],
            device,
        )

    rows_out = out_high.shape[0]
    last = (((1,), (1,)), ((), ()))

    def send_slab(slab):
        for step in range(width_col):
            peer_col = lax.rem(my_col + step, width_col)
            peer = slab * width_col + peer_col

            @pl.when(peer != me)
            def _(peer=peer, peer_col=peer_col):
                back_copy(peer, me, (slab, peer_col)).start()

    for step in range(width_gx):
        slab = lax.rem(my_gx + step, width_gx)
        high, low = split(plane_ref[slab].reshape(lanes, lanes))
        both = lax.dot_general(out_stack, high, last, preferred_element_type=F32)
        value = both[:rows_out] + both[rows_out:]
        value = value + lax.dot_general(out_high, low, last, preferred_element_type=F32)
        result_ref[pl.ds(slab * width_col, width_col)] = value.reshape(width_col, channels, lanes)
        if step > 0:
            send_slab(lax.rem(my_gx + step - 1, width_gx))
    send_slab(lax.rem(my_gx + width_gx - 1, width_gx))
    keep = pltpu.make_async_copy(result_ref.at[me], out_ref.at[me], own.at[2])
    keep.start()

    def finish_sends(step, carry):
        peer = lax.rem(me + step, count)
        for part in range(groups):
            spectrum_copy(part, peer, me, place(peer)).wait_send()
        return carry

    lax.fori_loop(1, count, finish_sends, 0)
    for step in range(1, width_col):
        peer = lax.rem(my_col + step, width_col)
        factor_copy(peer, my_col, (my_gx, peer)).wait_send()
        core_copy(peer, my_col, (my_gx, peer)).wait_send()

    def finish(step, carry):
        peer = lax.rem(me + step, count)
        back_copy(peer, me, place(peer)).wait_send()
        source = lax.rem(me + count - step, count)
        back_copy(source, source, (my_gx, my_col)).wait_recv()
        return carry

    lax.fori_loop(1, count, finish, 0)
    keep.wait()


def fused(
    grid_field, core, in_factor, out_factor, x_factor, z_factor, kx_reach, width_gx, width_col,
    rank_dev,
):
    channels, planes, grid_y, grid_z = grid_field.shape
    modes_x, rank_x = x_factor.shape
    modes_z, rank_z = z_factor.shape
    modes_y, rank_out = kx_reach.shape[0], out_factor.shape[1]
    y_table, z_table = forward_tables(grid_y, grid_z, modes_y, modes_z, planes)
    fore, back = x_tables(planes * width_gx, modes_x)
    picks = selectors(width_col, rank_x, rank_dev, rank_z, rank_out)
    count = width_gx * width_col
    lanes, wide = planes * 2 * modes_z, planes * 2 * grid_z
    ranks = width_col * rank_x * rank_dev
    group = 8
    groups = channels // group
    dma = pltpu.SemaphoreType.DMA
    tables = [jnp.asarray(t) for t in picks + [y_table, z_table, fore, back]]
    return pl.pallas_call(
        functools.partial(fused_kernel, width_gx, width_col),
        out_shape=jax.ShapeDtypeStruct((count, channels, lanes), F32),
        in_specs=[pl.BlockSpec(memory_space=pltpu.HBM)] + [VMEM] * (6 + len(tables)),
        out_specs=VMEM,
        scratch_shapes=[
            pltpu.VMEM(grid_field.shape, BF16),
            pltpu.VMEM((group * modes_y, wide), BF16),
            pltpu.VMEM((group * modes_y, wide), BF16),
            pltpu.VMEM((groups, modes_y, group, lanes), F32),
            pltpu.VMEM((groups, count, group, lanes), F32),
            pltpu.VMEM(core.shape, F32),
            pltpu.VMEM((3 * channels, lanes), F32),
            pltpu.VMEM((width_col, 3 * channels, lanes), F32),
            pltpu.VMEM((modes_z, 2 * planes * width_gx, ranks), F32),
            pltpu.VMEM((modes_z * 2 * modes_x, 2 * ranks), BF16),
            pltpu.VMEM((modes_z * 2 * modes_x, 2 * ranks), BF16),
            pltpu.VMEM((width_gx, modes_z, lanes // modes_z, lanes), F32),
            pltpu.VMEM((count, channels, lanes), F32),
            dma((channels,)),
            dma((groups, count)),
            dma((groups, count)),
            dma((width_col,)),
            dma((width_col,)),
            dma((width_col,)),
            dma((width_col,)),
            dma((count,)),
            dma((count,)),
            dma((3 + groups,)),
        ],
        compiler_params=pltpu.CompilerParams(
            collective_id=0, has_side_effects=True, vmem_limit_bytes=48 * 2**20
        ),
    )(grid_field, core, in_factor, out_factor, x_factor.T, z_factor.T, kx_reach.T, *tables)


def inverse_kernel(spec_ref, y_ref, z_high_ref, z_low_ref, out_ref, high_ref, low_ref):
    step = pl.program_id(0)
    modes_y, channels, lanes = spec_ref.shape
    block, planes, grid_z = out_ref.shape[0], out_ref.shape[1], out_ref.shape[3]
    group = 8
    for part in range(channels // group):

        @pl.when(step * block == part * group)
        def _(part=part):
            values = spec_ref[:, part * group : (part + 1) * group]
            values = jnp.swapaxes(values, 0, 1).reshape(-1, lanes)
            high, low = split(values)
            result = dot(high, z_high_ref[...]) + dot(high, z_low_ref[...])
            result = result + dot(low, z_high_ref[...])
            rows = slice(part * group * modes_y, (part + 1) * group * modes_y)
            high_ref[rows], low_ref[rows] = split(result)

    def tall(values, plane):
        at = 2 * plane * grid_z
        return [values[:, at : at + grid_z], values[:, at + grid_z : at + 2 * grid_z]]

    for local in range(block):
        first = (step * block + local) * modes_y
        rows = pl.ds(pl.multiple_of(first, modes_y), modes_y)
        high, low = high_ref[rows], low_ref[rows]
        stacks = []
        for plane in range(planes):
            high_part = tall(high, plane)
            stacks.append(jnp.concatenate(high_part + tall(low, plane) + high_part, 0))
        for plane in range(0, planes, 2):
            value = dot(y_ref[...], jnp.concatenate(stacks[plane : plane + 2], 1)).astype(BF16)
            out_ref[local, plane] = value[:, :grid_z]
            out_ref[local, plane + 1] = value[:, grid_z:]


def inverse(returned, planes, grid_y, grid_z, modes_z):
    modes_y, channels, _ = returned.shape
    y_table, z_high, z_low = inverse_tables(grid_y, grid_z, modes_y, modes_z, planes)
    wide = planes * 2 * grid_z
    block = 4
    return pl.pallas_call(
        inverse_kernel,
        grid=(channels // block,),
        in_specs=[
            pl.BlockSpec(returned.shape, lambda i: (0, 0, 0)),
            pl.BlockSpec(y_table.shape, lambda i: (0, 0)),
            pl.BlockSpec(z_high.shape, lambda i: (0, 0)),
            pl.BlockSpec(z_low.shape, lambda i: (0, 0)),
        ],
        out_specs=pl.BlockSpec((block, planes, grid_y, grid_z), lambda i: (i, 0, 0, 0)),
        out_shape=jax.ShapeDtypeStruct((channels, planes, grid_y, grid_z), BF16),
        scratch_shapes=[
            pltpu.VMEM((channels * modes_y, wide), BF16),
            pltpu.VMEM((channels * modes_y, wide), BF16),
        ],
    )(returned, jnp.asarray(y_table), jnp.asarray(z_high), jnp.asarray(z_low))


def row_device(
    grid_field, tucker_core, in_factor, out_factor, x_factor, y_factor, z_factor, kx_reach
):
    _, planes, grid_y, grid_z = grid_field.shape
    width_gx, width_col = lax.axis_size("gx"), lax.axis_size("col")
    rank_out = out_factor.shape[1]
    rank_dev, rank_x, rank_z = tucker_core.shape[1], x_factor.shape[1], z_factor.shape[1]
    y_rows = lax.dynamic_slice_in_dim(y_factor, lax.axis_index("gx") * width_col, width_col)
    core = jnp.einsum("prsabe,db->dpares", tucker_core, y_rows, precision=lax.Precision.HIGHEST)
    core = core.reshape(width_col, 2 * rank_x * rank_dev, rank_z * rank_out)
    returned = fused(
        grid_field, core, in_factor, out_factor, x_factor, z_factor, kx_reach, width_gx, width_col,
        rank_dev,
    )
    return inverse(returned, planes, grid_y, grid_z, z_factor.shape[0])


def per_device(
    grid_field, tucker_core, in_factor, out_factor, x_factor, y_factor, z_factor, kx_reach
):
    planes, grid_z = grid_field.shape[1], grid_field.shape[3]
    modes_y, modes_z = y_factor.shape[0], z_factor.shape[0]
    devices = lax.axis_size("gx") * lax.axis_size("col")
    ranks = in_factor.shape[1] * x_factor.shape[1]
    row_each = (
        devices == modes_y
        and planes == 4
        and grid_field.shape[0] % 8 == 0
        and grid_z == 128
        and planes * 2 * modes_z == 128
        and ranks == 256
        and out_factor.shape[1] * z_factor.shape[1] == 128
    )
    device = row_device if row_each else plain_device
    return device(
        grid_field, tucker_core, in_factor, out_factor, x_factor, y_factor, z_factor, kx_reach
    )


def solution(mesh):
    return jax.shard_map(
        per_device,
        mesh=mesh,
        in_specs=(
            P("col", "gx", None, None),
            P(None, "col", None, None, None, None),
            P("col", None),
            P("col", None),
            P(),
            P(),
            P(),
            P(),
        ),
        out_specs=P("col", "gx", None, None),
        check_vma=False,
    )
```

profile of v0, /device:TPU:0, one launch (start us, length us, event | category | flops | bytes accessed | tf_op | source)
XLA Modules:
  0.0 43.2 jit_solution(1065160529758356822)
XLA Ops:
  0.0 0.0 copy-start
  0.0 1.6 %copy-done = f32[2,8,32,8,8,4]{2,5,4,3,1,0:T(4,128)S(1)} copy-done((f32[2,8,32,8,8,4]{2,5,4,3,1,0:T(4,128)S(1)}, f32[2,8,32,8,8,4]{2,5,4,3,1,0:T(4,128)}, u32[]{:S(2)}) %copy-start) | copy-done | bytes 524312
  1.6 2.6 %fusion.2 = f32[4,2,8,8,4,32]{5,0,4,2,3,1:T(4,128)S(1)} fusion(f32[2,8,32,8,8,4]{2,5,4,3,1,0:T(4,128)S(1)} %copy-done, f32[32,8]{0,1:T(8,128)} %param.24, s32[]{:T(128)S(6)} %select_n.3), kind=kOutput, calls=%fused_computation.2 | convolution fusion | flops 6291456 | bytes 787460 | tf_op jit(solution)/shard_map/prsabe,db->dpares/dot_general | solution.py:545
  4.2 0.0 copy-start.3
  4.2 0.0 copy-start.4
  4.3 0.0 copy-start.5
  4.3 0.0 copy-start.6
  4.3 0.0 copy-start.7
  4.3 0.0 copy-start.8
  4.3 0.0 copy-start.9
  4.3 0.0 copy-start.10
  4.3 0.0 copy-start.11
  4.3 0.0 copy-start.12
  4.4 0.0 copy-start.13
  4.4 0.0 copy-start.14
  4.4 0.0 copy-start.15
  4.4 1.2 %copy.22 = f32[4,2,8,8,4,32]{5,4,3,2,1,0:T(4,128)} copy(f32[4,2,8,8,4,32]{5,0,4,2,3,1:T(4,128)S(1)} %fusion.2) | data formatting | bytes 524288 | tf_op jit(solution)/shard_map/prsabe,db->dpares/transpose | solution.py:545
  5.6 1.7 %reshape.3.core_ref = f32[4,128,128]{2,1,0:T(8,128)S(1)} reshape(f32[4,2,8,8,4,32]{5,4,3,2,1,0:T(4,128)} %copy.22) | data formatting | bytes 524288 | tf_op jit(solution)/shard_map/reshape | solution.py:546
  7.3 0.0 copy-done.3
  7.3 0.0 copy-done.4
  7.3 0.0 copy-done.5
  7.4 0.0 copy-done.6
  7.4 0.0 copy-done.7
  7.4 0.0 copy-done.8
  7.4 0.0 copy-done.9
  7.4 0.0 copy-done.10
  7.4 0.0 copy-done.11
  7.4 0.0 copy-done.12
  7.4 0.0 copy-done.13
  7.4 0.0 copy-done.14
  7.4 0.0 copy-done.15
  7.5 0.0 copy-start.1
  7.5 2.2 %copy-done.1 = bf16[16,4,256,128]{3,2,1,0:T(8,128)(2,1)S(1)} copy-done((bf16[16,4,256,128]{3,2,1,0:T(8,128)(2,1)S(1)}, bf16[16,4,256,128]{3,2,1,0:T(8,128)(2,1)}, u32[]{:S(2)}) %copy-start.1) | copy-done | bytes 4194328
  9.6 27.3 %shard_map.181.spec_ref = f32[32,16,128]{2,1,0:T(8,128)S(1)} custom-call(bf16[16,4,256,128]{3,2,1,0:T(8,128)(2,1)S(1)} %copy-done.1, f32[4,128,128]{2,1,0:T(8,128)S(1)} %reshape.3.core_ref, f32[16,32]{1,0:T(8,128)S(1)} %copy-done.9, f32[16,32]{1,0:T(8,128)S(1)} %copy-done.10, f32[8,32]{1,0:T(8,128)S(1)} %bitcast.12, f32[4,16]{1,0:T(4,128)S(1)} %bitcast.13, ...), custom_call_target="tpu_custom_call" | custom-call | tf_op jit(solution)/shard_map/pallas_call | solution.py:443
  36.9 0.0 copy-start.2
  36.9 0.7 %copy-done.2 = f32[32,16,128]{2,1,0:T(8,128)} copy-done((f32[32,16,128]{2,1,0:T(8,128)}, f32[32,16,128]{2,1,0:T(8,128)S(1)}, u32[]{:S(2)}) %copy-start.2) | copy-done | bytes 262168
  37.6 5.6 %shard_map.182 = bf16[16,4,256,128]{3,2,1,0:T(8,128)(2,1)} custom-call(f32[32,16,128]{2,1,0:T(8,128)} %copy-done.2, bf16[256,192]{1,0:T(8,128)(2,1)} %constant.42.clone.y_ref, bf16[128,1024]{1,0:T(8,128)(2,1)} %constant.43.clone.z_high_ref, bf16[128,1024]{1,0:T(8,128)(2,1)} %constant.44.clone.z_low_ref), custom_call_target="tpu_custom_call" | custom-call | tf_op jit(solution)/shard_map/pallas_call | solution.py:519
Async XLA Ops:
  0.0 1.6 %copy-start = (f32[2,8,32,8,8,4]{2,5,4,3,1,0:T(4,128)S(1)}, f32[2,8,32,8,8,4]{2,5,4,3,1,0:T(4,128)}, u32[]{:S(2)}) copy-start(f32[2,8,32,8,8,4]{2,5,4,3,1,0:T(4,128)} %param.20) | copy-start | bytes 1572868
  4.2 3.1 %copy-start.3 = (bf16[1024,256]{1,0:T(8,128)(2,1)S(1)}, bf16[1024,256]{1,0:T(8,128)(2,1)}, u32[]{:S(2)}) copy-start(bf16[1024,256]{1,0:T(8,128)(2,1)} %constant.39.clone.z_table_ref) | copy-start | bytes 1572868
  4.2 3.1 %copy-start.4 = (bf16[128,192]{1,0:T(8,128)(2,1)S(1)}, bf16[128,192]{1,0:T(8,128)(2,1)}, u32[]{:S(2)}) copy-start(bf16[128,192]{1,0:T(8,128)(2,1)} %constant.40.clone.fore_ref) | copy-start | bytes 147460
  4.3 3.1 %copy-start.5 = (bf16[128,256]{1,0:T(8,128)(2,1)S(1)}, bf16[128,256]{1,0:T(8,128)(2,1)}, u32[]{:S(2)}) copy-start(bf16[128,256]{1,0:T(8,128)(2,1)} %constant.38.clone.y_table_ref) | copy-start | bytes 196612
  4.3 3.1 %copy-start.6 = (bf16[64,192]{1,0:T(8,128)(2,1)S(1)}, bf16[64,192]{1,0:T(8,128)(2,1)}, u32[]{:S(2)}) copy-start(bf16[64,192]{1,0:T(8,128)(2,1)} %constant.41.clone.back_ref) | copy-start | bytes 73732
  4.3 3.1 %copy-start.7 = (f32[32,256]{1,0:T(8,128)S(1)}, f32[32,256]{1,0:T(8,128)}, u32[]{:S(2)}) copy-start(f32[32,256]{1,0:T(8,128)} %constant.35.clone.in_pick_ref) | copy-start | bytes 98308
  4.3 3.1 %copy-start.8 = (f32[32,128]{1,0:T(8,128)S(1)}, f32[32,128]{1,0:T(8,128)}, u32[]{:S(2)}) copy-start(f32[32,128]{1,0:T(8,128)} %constant.37.clone.out_pick_ref) | copy-start | bytes 49156
  4.3 3.1 %copy-start.9 = (f32[16,32]{1,0:T(8,128)S(1)}, f32[16,32]{1,0:T(8,128)}, u32[]{:S(2)}) copy-start(f32[16,32]{1,0:T(8,128)} %in_ref.1) | copy-start | bytes 6148
  4.3 3.1 %copy-start.10 = (f32[16,32]{1,0:T(8,128)S(1)}, f32[16,32]{1,0:T(8,128)}, u32[]{:S(2)}) copy-start(f32[16,32]{1,0:T(8,128)} %out_factor_ref.1) | copy-start | bytes 6148
  4.3 3.1 %copy-start.11 = (s32[32,16]{0,1:T(8,128)S(1)}, s32[32,16]{0,1:T(8,128)}, u32[]{:S(2)}) copy-start(s32[32,16]{0,1:T(8,128)} %param.26) | copy-start | bytes 6148
  4.3 3.1 %copy-start.12 = (f32[8,256]{1,0:T(8,128)S(1)}, f32[8,256]{1,0:T(8,128)}, u32[]{:S(2)}) copy-start(f32[8,256]{1,0:T(8,128)} %constant.34.clone.x_pick_ref) | copy-start | bytes 24580
  4.4 3.1 %copy-start.13 = (f32[32,8]{0,1:T(8,128)S(1)}, f32[32,8]{0,1:T(8,128)}, u32[]{:S(2)}) copy-start(f32[32,8]{0,1:T(8,128)} %param.23) | copy-start | bytes 3076
  4.4 3.1 %copy-start.14 = (f32[16,4]{0,1:T(4,128)S(1)}, f32[16,4]{0,1:T(4,128)}, u32[]{:S(2)}) copy-start(f32[16,4]{0,1:T(4,128)} %param.25) | copy-start | bytes 772
  4.4 3.1 %copy-start.15 = (f32[4,128]{1,0:T(4,128)S(1)}, f32[4,128]{1,0:T(4,128)}, u32[]{:S(2)}) copy-start(f32[4,128]{1,0:T(4,128)} %constant.36.clone.z_pick_ref) | copy-start | bytes 6148
  7.5 2.2 %copy-start.1 = (bf16[16,4,256,128]{3,2,1,0:T(8,128)(2,1)S(1)}, bf16[16,4,256,128]{3,2,1,0:T(8,128)(2,1)}, u32[]{:S(2)}) copy-start(bf16[16,4,256,128]{3,2,1,0:T(8,128)(2,1)} %field_ref.1) | copy-start | bytes 12582916
  36.9 0.7 %copy-start.2 = (f32[32,16,128]{2,1,0:T(8,128)}, f32[32,16,128]{2,1,0:T(8,128)S(1)}, u32[]{:S(2)}) copy-start(f32[32,16,128]{2,1,0:T(8,128)S(1)} %shard_map.181.spec_ref) | copy-start | bytes 786436
where the time goes:
time: 43.5 us; the launch traced here: 43.2 us
  Pallas kernels  32.8 us (75%)
  local copies, waits for them, and re-layouts  7.48 us (17%)
  matrix products  2.63 us (6%)
    pallas_call x1, Pallas kernels, fused(): pl.pallas_call(functools.partial(fused_kernel, width_gx, width_col), out_...  27.3 us
    pallas_call x1, Pallas kernels, inverse(): pl.pallas_call(inverse_kernel, grid=(channels // block,), in_specs=[pl.Bl...  5.57 us
    unnamed x32, local copies, waits for them, and re-layouts  4.55 us
    dot_general x1, matrix products, row_device(): jnp.einsum('prsabe,db->dpares', tucker_core, y_rows, precision=lax.Precis...  2.63 us
    reshape x1, local copies, waits for them, and re-layouts, row_device(): core = core.reshape(width_col, 2 * rank_x * rank_dev, rank_z * rank_out)  1.69 us
    transpose x1, local copies, waits for them, and re-layouts, row_device(): jnp.einsum('prsabe,db->dpares', tucker_core, y_rows, precision=lax.Precis...  1.24 us

commit v1 on v0

v1 whole, which is shorter than its diff:
```python
import functools
import math

import jax
import jax.numpy as jnp
import numpy as np
from jax import lax
from jax.experimental import pallas as pl
from jax.experimental.pallas import tpu as pltpu
from jax.sharding import PartitionSpec as P

MESH = pl.DeviceIdType.MESH
VMEM = pl.BlockSpec(memory_space=pltpu.VMEM)
F32 = jnp.float32
BF16 = jnp.bfloat16


def slot_freq(slot_count):
    slot_index = jnp.arange(slot_count, dtype=jnp.int32)
    return jnp.where(slot_index < slot_count // 2, slot_index, slot_index - slot_count)


def phase_table(positions, extent, slot_count, direction):
    phase_steps = positions[:, None] * slot_freq(slot_count)[None, :] % extent
    radians = 2.0 * math.pi / extent * phase_steps.astype(jnp.float32)
    norm_scale = 1.0 / math.sqrt(extent)
    cosine = jnp.cos(radians) * norm_scale
    sine_part = direction * jnp.sin(radians) * norm_scale
    return jnp.stack([jnp.stack([cosine, -sine_part], 1), jnp.stack([sine_part, cosine], 1)], 1)


def z_tables(grid_z, modes_z):
    z_index = jnp.arange(grid_z, dtype=jnp.int32)
    kz_index = jnp.arange(modes_z, dtype=jnp.int32)
    phase_steps = z_index[:, None] * kz_index[None, :] % grid_z
    radians = 2.0 * math.pi / grid_z * phase_steps.astype(jnp.float32)
    norm_scale = 1.0 / math.sqrt(grid_z)
    cosine = jnp.cos(radians) * norm_scale
    sine_part = jnp.sin(radians) * norm_scale
    forward = jnp.stack([cosine, -sine_part], 1)
    weight = jnp.where(kz_index == 0, 1.0, 2.0).astype(jnp.float32)
    backward = jnp.stack([(cosine * weight[None, :]).T, -(sine_part * weight[None, :]).T], 0)
    return (forward, backward)


def plain_device(
    grid_field, tucker_core, in_factor, out_factor, x_factor, y_factor, z_factor, kx_reach
):
    highest = lax.Precision.HIGHEST
    channels, planes, grid_y, grid_z = grid_field.shape
    modes_x = x_factor.shape[0]
    modes_y = y_factor.shape[0]
    modes_z = z_factor.shape[0]
    width_gx = lax.axis_size("gx")
    grid_x = planes * width_gx
    columns = modes_y * modes_z
    col_dev = columns // width_gx
    slab_index = lax.axis_index("gx")
    z_forward, z_backward = z_tables(grid_z, modes_z)
    y_forward = phase_table(jnp.arange(grid_y, dtype=jnp.int32), grid_y, modes_y, 1.0)
    x_forward = phase_table(jnp.arange(grid_x, dtype=jnp.int32), grid_x, modes_x, 1.0)
    values = grid_field.astype(jnp.float32)
    z_spectrum = jnp.einsum("cxyz,zpl->cxply", values, z_forward, precision=highest)
    y_spectrum = jnp.einsum("cxply,ypqj->qcxjl", z_spectrum, y_forward, precision=highest)
    y_spectrum = y_spectrum.reshape(2, channels, planes, columns)
    first_col = slab_index * col_dev
    reach_dev = lax.dynamic_slice_in_dim(kx_reach.reshape(-1), first_col, col_dev)
    kept_mask = (jnp.abs(slot_freq(modes_x))[:, None] < reach_dev[None, :]).astype(jnp.float32)
    arrived = lax.all_to_all(y_spectrum, "gx", split_axis=3, concat_axis=2, tiled=True)
    spectrum = jnp.einsum("pcxm,xpqk->qckm", arrived, x_forward, precision=highest)
    partial_value = jnp.einsum("qckm,cr->qrkm", spectrum, in_factor, precision=highest)
    amplitude = lax.psum_scatter(partial_value, "col", scatter_dimension=1, tiled=True)
    amplitude = amplitude * kept_mask[None, None]
    column = first_col + jnp.arange(col_dev, dtype=jnp.int32)
    pick_y = (column[:, None] // modes_z == jnp.arange(modes_y, dtype=jnp.int32)[None, :]).astype(
        jnp.float32
    )
    pick_z = (column[:, None] % modes_z == jnp.arange(modes_z, dtype=jnp.int32)[None, :]).astype(
        jnp.float32
    )
    y_rows = jnp.dot(pick_y, y_factor, precision=highest)
    z_rows = jnp.dot(pick_z, z_factor, precision=highest)
    core_cols = jnp.einsum("prsabe,mb,me->prsam", tucker_core, y_rows, z_rows, precision=highest)
    kernel = jnp.einsum("prsam,ka->prskm", core_cols, x_factor, precision=highest)
    mixed_re = jnp.einsum("rskm,rkm->skm", kernel[0], amplitude[0], precision=highest) - jnp.einsum(
        "rskm,rkm->skm", kernel[1], amplitude[1], precision=highest
    )
    mixed_im = jnp.einsum("rskm,rkm->skm", kernel[0], amplitude[1], precision=highest) + jnp.einsum(
        "rskm,rkm->skm", kernel[1], amplitude[0], precision=highest
    )
    mixed_sum = lax.psum(jnp.stack([mixed_re, mixed_im]), "col")
    out_spec = jnp.einsum("os,qskm->qokm", out_factor, mixed_sum, precision=highest)
    x_backward = phase_table(jnp.arange(grid_x, dtype=jnp.int32), grid_x, modes_x, -1.0)
    x_values = jnp.einsum("pckm,xpqk->qcxm", out_spec, x_backward, precision=highest)
    returned = lax.all_to_all(x_values, "gx", split_axis=2, concat_axis=3, tiled=True)
    returned = returned.reshape(2, channels, planes, modes_y, modes_z)
    y_backward = phase_table(jnp.arange(grid_y, dtype=jnp.int32), grid_y, modes_y, -1.0)
    y_values = jnp.einsum("pcxjl,ypqj->cxqly", returned, y_backward, precision=highest)
    result = jnp.einsum("cxqly,qlz->cxyz", y_values, z_backward, precision=highest)
    return result.astype(jnp.bfloat16)


def split_np(table):
    high = table.astype(np.float32).astype(BF16)
    low = (table - high.astype(np.float64)).astype(np.float32).astype(BF16)
    return high, low


def split(values):
    high = values.astype(BF16)
    return high, (values - high.astype(F32)).astype(BF16)


def freqs(slots):
    index = np.arange(slots)
    return np.where(index < slots // 2, index, index - slots)


def waves(extent, frequencies):
    steps = np.arange(extent)[:, None] * frequencies[None, :] % extent
    angle = 2.0 * np.pi / extent * steps
    return np.cos(angle) / math.sqrt(extent), np.sin(angle) / math.sqrt(extent)


def dot(a, b):
    return jnp.dot(a, b, preferred_element_type=F32)


def forward_tables(grid_y, grid_z, modes_y, modes_z, planes):
    cos_y, sin_y = waves(grid_y, freqs(modes_y))
    high, low = split_np(np.concatenate([cos_y.T, -sin_y.T], 0))
    y_table = np.concatenate([high, low], 0)
    cos_z, sin_z = waves(grid_z, np.arange(modes_z))
    table = np.zeros((planes, 2, grid_z, modes_z, planes, 2))
    for plane in range(planes):
        table[plane, 0, :, :, plane, 0] = cos_z
        table[plane, 0, :, :, plane, 1] = -sin_z
        table[plane, 1, :, :, plane, 0] = sin_z
        table[plane, 1, :, :, plane, 1] = cos_z
    high, low = split_np(table.reshape(planes * 2 * grid_z, -1))
    return y_table, np.concatenate([high, low], 1)


def inverse_tables(grid_y, grid_z, modes_y, modes_z, planes, halves):
    cos_y, sin_y = waves(grid_y, freqs(modes_y))
    high, low = split_np(np.concatenate([cos_y, -sin_y], 1))
    y_table = np.concatenate([high, high, low], 1)
    cos_z, sin_z = waves(grid_z, np.arange(modes_z))
    weight = np.where(np.arange(modes_z) == 0, 1.0, 2.0)
    cos_z, sin_z = (cos_z * weight).T, (sin_z * weight).T
    table = np.zeros((modes_z, planes, 2, planes, 2, grid_z))
    for plane in range(planes):
        table[:, plane, 0, plane, 0, :] = cos_z
        table[:, plane, 1, plane, 0, :] = -sin_z
        table[:, plane, 0, plane, 1, :] = sin_z
        table[:, plane, 1, plane, 1, :] = cos_z
    high, low = split_np(table.reshape(halves, modes_z // halves * planes * 2, -1))
    return y_table, np.concatenate([high, high, low], 1)


def x_tables(grid_x, modes_x):
    cos_x, sin_x = waves(grid_x, freqs(modes_x))
    real = np.stack([cos_x.T, sin_x.T], 2).reshape(modes_x, -1)
    imag = np.stack([-sin_x.T, cos_x.T], 2).reshape(modes_x, -1)
    high, low = split_np(np.concatenate([real, imag, -imag, real], 0))
    forward = np.concatenate([high, high, low], 1)
    real = np.concatenate([cos_x, -sin_x], 1)
    imag = np.concatenate([sin_x, cos_x], 1)
    high, low = split_np(np.stack([real, imag], 1).reshape(grid_x * 2, -1))
    backward = np.concatenate([high, high, low], 1)
    return forward, backward


def selectors(width_col, rank_in, rank_x, rank_y, rank_z, rank_out):
    wide = np.arange(rank_in * rank_x)
    x_pick = wide % rank_x == np.arange(rank_x)[:, None]
    in_pick = wide // rank_x == np.arange(rank_in)[:, None]
    slim = np.arange(rank_z * rank_out)
    z_pick = slim // rank_out == np.arange(rank_z)[:, None]
    out_pick = slim % rank_out == np.arange(rank_out)[:, None]
    core_in = np.arange(rank_x * rank_y * rank_z)
    y_pick = core_in // rank_z % rank_y == np.arange(rank_y)[:, None]
    core_out = np.arange(rank_z * width_col * rank_x)
    same_x = core_in // (rank_y * rank_z) == core_out[:, None] % rank_x
    same_z = core_in % rank_z == core_out[:, None] // (width_col * rank_x)
    picks = (x_pick, in_pick, z_pick, out_pick, y_pick, same_x & same_z)
    return [pick.astype(np.float32) for pick in picks]


def spread(values, pick, dim):
    return lax.dot_general(
        values, pick, (((dim,), (0,)), ((), ())), precision=lax.Precision.HIGHEST,
        preferred_element_type=F32,
    )


HALVES = 2


def fused_kernel(
    width_gx, width_col, field_hbm, core_hbm, in_hbm, out_hbm, x_hbm, y_hbm, z_hbm, reach_hbm,
    x_pick_hbm, in_pick_hbm, z_pick_hbm, out_pick_hbm, y_pick_hbm, same_hbm, y_table_hbm,
    z_table_hbm, fore_hbm, back_hbm, z_back_hbm, y_back_hbm, high_out, low_out, y_back_ref, field,
    core_in, in_ref, out_ref, x_ref, y_ref, z_ref, reach_ref, x_pick_ref, in_pick_ref, z_pick_ref,
    out_pick_ref, y_pick_ref, same_ref, y_table_ref, z_table_ref, fore_ref, back_ref, z_back_ref,
    y_high, y_low, values_ref, spec, arrived, cores, cores_in, factor, factors, kept_ref, rank_ref,
    high_ref, low_ref, plane_ref, result, returned, partial_ref, field_sems, load_sems, sends, recvs,
    core_sends, core_recvs, factor_sends, factor_recvs, back_sends, back_recvs,
):
    count = width_gx * width_col
    my_gx, my_col = lax.axis_index("gx"), lax.axis_index("col")
    me = my_gx * width_col + my_col
    channels, planes, _, grid_z = field.shape
    _, modes_y, group, lanes = spec.shape
    modes_x, modes_z = x_ref.shape[1], z_ref.shape[1]
    barrier = pltpu.get_barrier_semaphore()
    gx_steps = sorted(range(width_gx), key=lambda step: min(step, width_gx - step))
    col_steps = range(width_col)

    def slab_at(step):
        return lax.rem(my_gx + step, width_gx)

    def col_at(step):
        return lax.rem(my_col + step, width_col)

    for gx_step in gx_steps:
        for col_step in col_steps:
            if gx_step or col_step:
                pl.semaphore_signal(
                    barrier, inc=1, device_id=(slab_at(gx_step), col_at(col_step)),
                    device_id_type=MESH,
                )

    def fetch(channel):
        return pltpu.make_async_copy(
            field_hbm.at[channel], field.at[channel], field_sems.at[channel]
        )

    sources = [
        y_table_hbm, z_table_hbm, core_hbm, y_hbm, y_pick_hbm, same_hbm, in_hbm, out_hbm,
        in_pick_hbm, out_pick_hbm, x_hbm, z_hbm, reach_hbm, x_pick_hbm, z_pick_hbm, fore_hbm,
        back_hbm, z_back_hbm, y_back_hbm,
    ]
    targets = [
        y_table_ref, z_table_ref, core_in, y_ref, y_pick_ref, same_ref, in_ref, out_ref,
        in_pick_ref, out_pick_ref, x_ref, z_ref, reach_ref, x_pick_ref, z_pick_ref, fore_ref,
        back_ref, z_back_ref, y_back_ref,
    ]
    loads = [
        pltpu.make_async_copy(source, target, load_sems.at[index])
        for index, (source, target) in enumerate(zip(sources, targets))
    ]
    loads[0].start()

    def begin(channel, carry):
        fetch(channel).start()
        return carry

    lax.fori_loop(0, channels, begin, 0)
    for load in loads[1:]:
        load.start()

    def remote(source, target, send_sem, recv_sem, device):
        return pltpu.make_async_remote_copy(
            src_ref=source, dst_ref=target, send_sem=send_sem, recv_sem=recv_sem,
            device_id=device, device_id_type=MESH,
        )

    loads[0].wait()
    half = 2 * modes_y
    pair = 2
    for part in range(HALVES):

        def transform(step, carry, part=part):
            for offset in range(pair):
                local = step * pair + offset
                channel = part * group + local
                fetch(channel).wait()
                parts = []
                for plane in range(planes):
                    both = dot(y_table_ref[...], field[channel, plane])
                    y_values = both[:half] + both[half:]
                    parts += [y_values[:modes_y], y_values[modes_y:]]
                high, low = split(jnp.concatenate(parts, 1))
                rows = pl.ds(pl.multiple_of(local * modes_y, modes_y), modes_y)
                y_high[rows] = high
                y_low[rows] = low
            return carry

        lax.fori_loop(0, group // pair, transform, 0)
        if part == 0:
            loads[1].wait()
        both = dot(y_high[...], z_table_ref[...])
        value = both[:, :lanes] + both[:, lanes:] + dot(y_low[...], z_table_ref[:, :lanes])
        values_ref[part] = jnp.swapaxes(value.reshape(group, modes_y, lanes), 0, 1)

    spot = lax.broadcasted_iota(jnp.int32, (modes_y, group, lanes), 2)
    first, second = values_ref[0], values_ref[1]
    middle = lanes // HALVES
    spec[0] = jnp.where(spot < middle, first, pltpu.roll(second, middle, 2))
    spec[1] = jnp.where(spot < middle, pltpu.roll(first, middle, 2), second)

    for load in loads[2:10]:
        load.wait()
    rank_out = in_ref.shape[1]
    factor[...] = jnp.concatenate(
        [in_ref[...], out_ref[...], jnp.zeros((channels, lanes - 2 * rank_out), F32)], 1
    )
    y_wide = spread(y_ref[...], y_pick_ref[...], 0)
    row = lax.broadcasted_iota(jnp.int32, (same_ref.shape[0], y_wide.shape[0]), 0)
    spot = lax.broadcasted_iota(jnp.int32, row.shape, 1)
    rank_x = x_ref.shape[0]
    wanted = my_gx * width_col + lax.rem(lax.div(row, rank_x), width_col)
    y_high_rows, y_low_rows = split(
        spread(jnp.where(spot == wanted, 1.0, 0.0), y_wide, 1) * same_ref[...]
    )
    y_stack = jnp.concatenate([y_high_rows, y_low_rows], 0)
    core_rows = y_wide.shape[1]
    out_rows = same_ref.shape[0]
    rank_z = lanes // rank_out
    spot_rows = width_col * rank_x

    def contract(step, carry):
        rows = pl.ds(pl.multiple_of(step * core_rows, core_rows), core_rows)
        high, low = split(core_in[rows])
        both = dot(y_stack, high)
        value = both[:out_rows] + both[out_rows:] + dot(y_high_rows, low)
        wide = jnp.concatenate(
            [value[e * spot_rows : (e + 1) * spot_rows] for e in range(rank_z)], 1
        )
        place = pl.ds(pl.multiple_of(step * rank_x, rank_x), rank_x)
        for target in range(width_col):
            cores[target, place] = wide[target * rank_x : (target + 1) * rank_x]
        return carry

    lax.fori_loop(0, core_in.shape[0] // core_rows, contract, 0)

    pl.semaphore_wait(barrier, count - 1)

    def factor_copy(writer, device):
        return remote(
            factor, factors.at[writer], factor_sends.at[0], factor_recvs.at[writer], device
        )

    def core_copy(peer, writer, device):
        return remote(
            cores.at[peer], cores_in.at[writer], core_sends.at[0], core_recvs.at[writer], device
        )

    def send_half(part, source, target, send_sems, recv_sems):
        for gx_step in gx_steps:
            slab = slab_at(gx_step)
            for col_step in col_steps:
                if gx_step or col_step:
                    column = col_at(col_step)
                    remote(
                        source.at[part, slab * width_col + column], target.at[part, me],
                        send_sems.at[part], recv_sems.at[part, my_gx], (slab, column),
                    ).start()

    def receive(part, target, recv_sems, slab, messages):
        block = target.at[part, pl.ds(0, messages)]
        remote(block, block, recv_sems.at[part, slab], recv_sems.at[part, slab], (my_gx, my_col)
               ).wait_recv()

    for step in range(1, width_col):
        factor_copy(my_col, (my_gx, col_at(step))).start()
    send_half(0, spec, arrived, sends, recvs)
    for step in range(1, width_col):
        core_copy(col_at(step), my_col, (my_gx, col_at(step))).start()
    send_half(1, spec, arrived, sends, recvs)

    for part in range(HALVES):
        arrived[part, me] = spec[part, me]
    cores_in[my_col] = cores[my_col]
    factors[my_col] = factor[...]
    for load in loads[10:17]:
        load.wait()
    x_wide = spread(x_ref[...], x_pick_ref[...], 0)
    z_rows = spread(z_ref[...], z_pick_ref[...], 0)
    spot = lax.broadcasted_iota(jnp.int32, reach_ref.shape, 1)
    reach = jnp.where(spot == me, reach_ref[...].astype(F32), 0.0)
    reach = jnp.sum(reach, axis=1, keepdims=True)
    slot = lax.broadcasted_iota(jnp.int32, x_wide.shape, 0)
    slot = jnp.where(slot < modes_x // 2, slot, modes_x - slot).astype(F32)
    for l in range(modes_z):
        kept_ref[l] = jnp.where(slot < reach[l : l + 1], x_wide, 0.0)

    for step in range(1, width_col):
        factor_copy(col_at(step), (my_gx, my_col)).wait_recv()
    in_stack, out_parts = [], []
    for part in range(HALVES):
        rows = factors[:, part * group : (part + 1) * group].reshape(width_col * group, lanes)
        in_high, in_low = split(spread(rows[:, :rank_out], in_pick_ref[...], 1))
        in_stack += [in_high, in_low, in_high, in_low]
        out_parts.append(spread(rows[:, rank_out : 2 * rank_out], out_pick_ref[...], 1))
    in_stack = jnp.concatenate(in_stack, 0)
    out_high, out_low = split(jnp.concatenate(out_parts, 0))
    out_stack = jnp.concatenate([out_high, out_low], 0)
    rows_out = out_high.shape[0]

    lead = 2 * planes
    modes_half = modes_z // HALVES
    both_modes = 2 * modes_x
    ranks = x_wide.shape[1]
    last = (((1,), (1,)), ((), ()))

    def gather_ranks(part):
        for gx_step in gx_steps:
            slab = slab_at(gx_step)
            receive(part, arrived, recvs, slab, width_col if gx_step else width_col - 1)
            block = arrived[part, pl.ds(slab * width_col, width_col)]
            block = block.reshape(width_col * group, lanes)
            high = block.astype(BF16).astype(F32)
            low = block - high
            stacked = jnp.concatenate([high, high, low, low], 0).T.astype(BF16)
            wide = jnp.concatenate([stacked[:middle], stacked[middle:]], 1)
            value = dot(wide, in_stack).reshape(modes_half, lead, ranks)
            rank_ref[:, pl.ds(pl.multiple_of(slab * lead, lead), lead)] = value

    def mix(part, core_high, core_both):
        for l in range(modes_half):
            high, low = split(rank_ref[l])
            value = dot(fore_ref[...], jnp.concatenate([high, low, high], 0))
            kept = kept_ref[part * modes_half + l]
            value = value * jnp.concatenate([kept] * 4, 0)
            value = jnp.concatenate([value[:both_modes], value[both_modes:]], 1)
            rows = slice(l * both_modes, (l + 1) * both_modes)
            high_ref[rows], low_ref[rows] = split(value)
        both = dot(high_ref[...], core_both)
        mixed = both[:, :lanes] + both[:, lanes:] + dot(low_ref[...], core_high)
        for l in range(modes_half):
            at = part * modes_half + l
            value = mixed[l * both_modes : (l + 1) * both_modes] * z_rows[at : at + 1]
            high, low = split(value)
            value = dot(back_ref[...], jnp.concatenate([high, low, high], 0))
            plane_ref[:, l] = value.reshape(width_gx, lead, lanes)

    def expand(part):
        spot = lax.broadcasted_iota(jnp.int32, (rows_out // HALVES, lanes), 1)
        for slab in range(0, width_gx, HALVES):
            rows = plane_ref[slab : slab + HALVES].reshape(lanes, lanes)
            high, low = split(rows)
            both = lax.dot_general(out_stack, high, last, preferred_element_type=F32)
            value = both[:rows_out] + both[rows_out:]
            value = value + lax.dot_general(out_high, low, last, preferred_element_type=F32)
            first, second = value[: rows_out // HALVES], value[rows_out // HALVES :]
            pieces = (
                jnp.where(spot < middle, first, pltpu.roll(second, middle, 1)),
                jnp.where(spot < middle, pltpu.roll(first, middle, 1), second),
            )
            for offset, piece in enumerate(pieces):
                at = (slab + offset) * width_col
                result[part, at : at + width_col] = piece.reshape(width_col, group, lanes)

    for part in range(HALVES):
        gather_ranks(part)
        if part == 0:
            for step in range(1, width_col):
                core_copy(my_col, col_at(step), (my_gx, my_col)).wait_recv()
            half_rows = cores.shape[1] // 2
            core = [cores_in[:, first : first + half_rows] for first in (0, half_rows)]
            core = jnp.concatenate([rows.reshape(ranks, lanes) for rows in core], 0)
            core_high, core_low = split(core)
            core_both = jnp.concatenate([core_high, core_low], 1)
        mix(part, core_high, core_both)
        expand(part)
        send_half(part, result, returned, back_sends, back_recvs)
        returned[part, me] = result[part, me]

    loads[17].wait()
    ky_half = modes_y // 2
    gx_half = width_gx // 2
    my_half = lax.div(my_gx, gx_half)
    spot = lax.broadcasted_iota(jnp.int32, (group * ky_half, lanes), 1)
    wide = 2 * grid_z
    for part in range(HALVES):
        for turn in range(2):
            side = lax.rem(my_half + turn, 2)
            for step in range(gx_half):
                slab = side * gx_half + lax.rem(my_gx + step, gx_half)
                full = turn > 0 or step > 0
                receive(part, returned, back_recvs, slab, width_col if full else width_col - 1)
            block = returned[part, pl.ds(side * ky_half, ky_half)]
            block = jnp.swapaxes(block, 0, 1).reshape(group * ky_half, lanes)
            high = block.astype(BF16).astype(F32)
            low = block - high
            high_turned, low_turned = pltpu.roll(high, middle, 1), pltpu.roll(low, middle, 1)
            one = [jnp.where(spot < middle, high, low_turned), high[:, :middle]]
            two = [jnp.where(spot < middle, high_turned, low), high_turned[:, :middle]]
            stacked = jnp.concatenate(
                [jnp.concatenate(one, 1), jnp.concatenate(two, 1)], 0
            ).astype(BF16)
            rows = pl.ds(pl.multiple_of(side * ky_half, ky_half), ky_half)
            for plane in range(planes):
                at = slice(plane * wide, (plane + 1) * wide)
                value = dot(stacked, z_back_ref[part, :, at]).reshape(channels, ky_half, wide)
                if part + 1 < HALVES:
                    partial_ref[:, rows, at] = value
                else:
                    value = value + partial_ref[:, rows, at]
                    high_out[:, rows, at], low_out[:, rows, at] = split(value)

    loads[18].wait()
    for source, send_sem in ((factors, factor_sends.at[0]), (cores, core_sends.at[0])):
        block = source.at[pl.ds(0, width_col - 1)]
        remote(block, block, send_sem, send_sem, (my_gx, my_col)).wait_send()
    for part in range(HALVES):
        for target, send_sems in ((spec, sends), (result, back_sends)):
            block = target.at[part, pl.ds(0, count - 1)]
            remote(block, block, send_sems.at[part], send_sems.at[part], (my_gx, my_col)
                   ).wait_send()


def fused(
    grid_field, core, in_factor, out_factor, x_factor, y_factor, z_factor, kx_reach, width_gx,
    width_col,
):
    channels, planes, grid_y, grid_z = grid_field.shape
    modes_x, rank_x = x_factor.shape
    modes_y, rank_y = y_factor.shape
    modes_z, rank_z = z_factor.shape
    rank_in, rank_out = in_factor.shape[1], out_factor.shape[1]
    y_table, z_table = forward_tables(grid_y, grid_z, modes_y, modes_z, planes)
    y_back, z_back = inverse_tables(grid_y, grid_z, modes_y, modes_z, planes, HALVES)
    fore, back = x_tables(planes * width_gx, modes_x)
    picks = selectors(width_col, rank_in, rank_x, rank_y, rank_z, rank_out)
    count = width_gx * width_col
    lanes, wide = planes * 2 * modes_z, planes * 2 * grid_z
    ranks = rank_in * rank_x
    group = channels // HALVES
    dma = pltpu.SemaphoreType.DMA
    tables = [jnp.asarray(t) for t in picks + [y_table, z_table, fore, back, z_back, y_back]]
    small = [in_factor, out_factor, x_factor.T, y_factor.T, z_factor.T, kx_reach.T]
    operands = [grid_field, core] + small + tables
    core_rows = 2 * rank_in // width_col * rank_x
    exchange = (HALVES, count, group, lanes)
    return pl.pallas_call(
        functools.partial(fused_kernel, width_gx, width_col),
        out_shape=[
            pltpu.VMEM((channels, modes_y, wide), BF16),
            pltpu.VMEM((channels, modes_y, wide), BF16),
            pltpu.VMEM(y_back.shape, BF16),
        ],
        in_specs=[pl.BlockSpec(memory_space=pltpu.HBM)] * len(operands),
        out_specs=[VMEM] * 3,
        scratch_shapes=[pltpu.VMEM(a.shape, a.dtype) for a in operands[:-1]]
        + [
            pltpu.VMEM((group * modes_y, wide), BF16),
            pltpu.VMEM((group * modes_y, wide), BF16),
            pltpu.VMEM((HALVES, modes_y, group, lanes), F32),
            pltpu.VMEM(exchange, F32),
            pltpu.VMEM(exchange, F32),
            pltpu.VMEM((width_col, core_rows, lanes), F32),
            pltpu.VMEM((width_col, core_rows, lanes), F32),
            pltpu.VMEM((channels, lanes), F32),
            pltpu.VMEM((width_col, channels, lanes), F32),
            pltpu.VMEM((modes_z, modes_x, ranks), F32),
            pltpu.VMEM((modes_z // HALVES, 2 * planes * width_gx, ranks), F32),
            pltpu.VMEM((modes_z // HALVES * 2 * modes_x, 2 * ranks), BF16),
            pltpu.VMEM((modes_z // HALVES * 2 * modes_x, 2 * ranks), BF16),
            pltpu.VMEM((width_gx, modes_z // HALVES, 2 * planes, lanes), F32),
            pltpu.VMEM(exchange, F32),
            pltpu.VMEM(exchange, F32),
            pltpu.VMEM((channels, modes_y, wide), F32),
            dma((channels,)),
            dma((len(operands) - 1,)),
            dma((HALVES,)),
            dma((HALVES, width_gx)),
            dma((1,)),
            dma((width_col,)),
            dma((1,)),
            dma((width_col,)),
            dma((HALVES,)),
            dma((HALVES, width_gx)),
        ],
        compiler_params=pltpu.CompilerParams(
            collective_id=0, has_side_effects=True, vmem_limit_bytes=VMEM_BYTES
        ),
    )(*[pltpu.with_memory_space_constraint(a, pltpu.HBM) for a in operands])


VMEM_BYTES = 40 * 2**20
INVERSE_BYTES = 16 * 2**20


def inverse_kernel(high_ref, low_ref, y_ref, out_hbm, out, sems):
    channels, planes, _, grid_z = out.shape

    def tall(values, plane):
        at = 2 * plane * grid_z
        return [values[:, at : at + grid_z], values[:, at + grid_z : at + 2 * grid_z]]

    def leave(channel):
        return pltpu.make_async_copy(out.at[channel], out_hbm.at[channel], sems.at[channel])

    def transform(channel, carry):
        high, low = high_ref[channel], low_ref[channel]
        stacks = []
        for plane in range(planes):
            high_part = tall(high, plane)
            stacks.append(jnp.concatenate(high_part + tall(low, plane) + high_part, 0))
        for plane in range(0, planes, 2):
            value = dot(y_ref[...], jnp.concatenate(stacks[plane : plane + 2], 1)).astype(BF16)
            out[channel, plane] = value[:, :grid_z]
            out[channel, plane + 1] = value[:, grid_z:]
        leave(channel).start()
        return carry

    lax.fori_loop(0, channels, transform, 0)

    def finish(channel, carry):
        leave(channel).wait()
        return carry

    lax.fori_loop(0, channels, finish, 0)


def inverse(high, low, y_table, shape):
    return pl.pallas_call(
        inverse_kernel,
        in_specs=[VMEM] * 3,
        out_specs=pl.BlockSpec(memory_space=pltpu.HBM),
        out_shape=jax.ShapeDtypeStruct(shape, BF16),
        scratch_shapes=[pltpu.VMEM(shape, BF16), pltpu.SemaphoreType.DMA((shape[0],))],
        compiler_params=pltpu.CompilerParams(vmem_limit_bytes=INVERSE_BYTES),
    )(*[pltpu.with_memory_space_constraint(a, pltpu.VMEM) for a in (high, low, y_table)])


def row_device(
    grid_field, tucker_core, in_factor, out_factor, x_factor, y_factor, z_factor, kx_reach
):
    width_gx, width_col = lax.axis_size("gx"), lax.axis_size("col")
    rank_out = out_factor.shape[1]
    core = jnp.transpose(tucker_core, (0, 1, 3, 4, 5, 2)).reshape(-1, rank_out)
    high, low, y_table = fused(
        grid_field, core, in_factor, out_factor, x_factor, y_factor, z_factor, kx_reach, width_gx,
        width_col,
    )
    return inverse(high, low, y_table, grid_field.shape)


def per_device(
    grid_field, tucker_core, in_factor, out_factor, x_factor, y_factor, z_factor, kx_reach
):
    planes, grid_z = grid_field.shape[1], grid_field.shape[3]
    modes_y, modes_z = y_factor.shape[0], z_factor.shape[0]
    devices = lax.axis_size("gx") * lax.axis_size("col")
    ranks = in_factor.shape[1] * x_factor.shape[1]
    row_each = (
        devices == modes_y
        and planes == 4
        and grid_field.shape[0] == 16
        and grid_z == 128
        and planes * 2 * modes_z == 128
        and ranks == 256
        and x_factor.shape[1] == 8
        and in_factor.shape[1] == out_factor.shape[1]
        and y_factor.shape[1] * x_factor.shape[1] * z_factor.shape[1] == 256
        and out_factor.shape[1] * z_factor.shape[1] == 128
    )
    device = row_device if row_each else plain_device
    return device(
        grid_field, tucker_core, in_factor, out_factor, x_factor, y_factor, z_factor, kx_reach
    )


def solution(mesh):
    return jax.shard_map(
        per_device,
        mesh=mesh,
        in_specs=(
            P("col", "gx", None, None),
            P(None, "col", None, None, None, None),
            P("col", None),
            P("col", None),
            P(),
            P(),
            P(),
            P(),
        ),
        out_specs=P("col", "gx", None, None),
        check_vma=False,
    )
```

time: 43.5 us -> 36 us (0.83)
  local copies, waits for them, and re-layouts: 7.48 us -> 0 us
  Pallas kernels: 32.8 us -> 35.8 us
  matrix products: 2.63 us -> 0 us
    unnamed x32 -> x0, local copies, waits for them, and re-layouts: 4.55 us -> none
    pallas_call x1, Pallas kernels: 27.3 us -> 31.4 us  [fused(): pl.pallas_call(functools.partial(fused_kernel, width_gx, width_col), out_...]
    dot_general x1 -> x0, matrix products: 2.63 us -> none  [row_device(): jnp.einsum('prsabe,db->dpares', tucker_core, y_rows, precision=lax.Precis...]
    reshape x1 -> x0, local copies, waits for them, and re-layouts: 1.69 us -> none  [row_device(): core = core.reshape(width_col, 2 * rank_x * rank_dev, rank_z * rank_out)]
    transpose x1 -> x0, local copies, waits for them, and re-layouts: 1.24 us -> none  [row_device(): jnp.einsum('prsabe,db->dpares', tucker_core, y_rows, precision=lax.Precis...]
    pallas_call x1, Pallas kernels: 5.57 us -> 4.42 us  [inverse(): pl.pallas_call(inverse_kernel, in_specs=[VMEM] * 3, out_specs=pl.BlockSpe...]
where the time goes in v1:
time: 36 us; the launch traced here: 35.8 us
  Pallas kernels  35.8 us (99%)
    pallas_call x1, Pallas kernels, fused(): pl.pallas_call(functools.partial(fused_kernel, width_gx, width_col), out_...  31.4 us
    pallas_call x1, Pallas kernels, inverse(): pl.pallas_call(inverse_kernel, in_specs=[VMEM] * 3, out_specs=pl.BlockSpe...  4.42 us

profile of v1, /device:TPU:0, one launch (start us, length us, event | category | flops | bytes accessed | tf_op | source)
XLA Modules:
  0.0 35.8 jit_solution(1245172777393338288)
XLA Ops:
  0.0 31.4 %shard_map.190 = (bf16[16,32,1024]{2,1,0:T(8,128)(2,1)S(1)}, bf16[16,32,1024]{2,1,0:T(8,128)(2,1)S(1)}, bf16[256,192]{1,0:T(8,128)(2,1)S(1)}) custom-call(bf16[16,4,256,128]{3,2,1,0:T(8,128)(2,1)} %field_hbm.1, f32[4096,32]{1,0:T(8,128)} %bitcast.7, f32[16,32]{1,0:T(8,128)} %in_hbm.1, f32[16,32]{1,0:T(8,128)} %out_hbm.1, f32[8,32]{1,0:T(8,128)} %bitcast.9, ...), custom_call_target="tpu_custom_call" | custom-call | tf_op jit(solution)/shard_map/pallas_call | solution.py:538
  31.4 4.4 %shard_map.191 = bf16[16,4,256,128]{3,2,1,0:T(8,128)(2,1)} custom-call(bf16[16,32,1024]{2,1,0:T(8,128)(2,1)S(1)} %get-tuple-element.8.high_ref, bf16[16,32,1024]{2,1,0:T(8,128)(2,1)S(1)} %get-tuple-element.9.low_ref, bf16[256,192]{1,0:T(8,128)(2,1)S(1)} %get-tuple-element.10.y_ref), custom_call_target="tpu_custom_call" | custom-call | tf_op jit(solution)/shard_map/pallas_call | solution.py:620

commit v2 on v1

--- a/solution.py
+++ b/solution.py
@@ -141,7 +141,7 @@
     return y_table, np.concatenate([high, low], 1)
 
 
-def inverse_tables(grid_y, grid_z, modes_y, modes_z, planes, halves):
+def inverse_tables(grid_y, grid_z, modes_y, modes_z, planes):
     cos_y, sin_y = waves(grid_y, freqs(modes_y))
     high, low = split_np(np.concatenate([cos_y, -sin_y], 1))
     y_table = np.concatenate([high, high, low], 1)
@@ -154,15 +154,19 @@
         table[:, plane, 1, plane, 0, :] = -sin_z
         table[:, plane, 0, plane, 1, :] = sin_z
         table[:, plane, 1, plane, 1, :] = cos_z
-    high, low = split_np(table.reshape(halves, modes_z // halves * planes * 2, -1))
-    return y_table, np.concatenate([high, high, low], 1)
+    high, low = split_np(table.reshape(modes_z, planes * 2, -1))
+    z_tables = []
+    for first, modes in mode_chunks(modes_z):
+        parts = [part[first : first + modes] for part in (high, high, low)]
+        z_tables.append(np.concatenate(parts, 0).reshape(3 * modes * planes * 2, -1))
+    return y_table, z_tables
 
 
 def x_tables(grid_x, modes_x):
     cos_x, sin_x = waves(grid_x, freqs(modes_x))
     real = np.stack([cos_x.T, sin_x.T], 2).reshape(modes_x, -1)
     imag = np.stack([-sin_x.T, cos_x.T], 2).reshape(modes_x, -1)
-    high, low = split_np(np.concatenate([real, imag, -imag, real], 0))
+    high, low = split_np(np.concatenate([real, imag], 0))
     forward = np.concatenate([high, high, low], 1)
     real = np.concatenate([cos_x, -sin_x], 1)
     imag = np.concatenate([sin_x, cos_x], 1)
@@ -194,27 +198,56 @@
     )
 
 
-HALVES = 2
+SHARES = (1, 1)
+
+
+def mode_chunks(modes_z):
+    sizes = [share * modes_z // sum(SHARES) for share in SHARES]
+    return [(sum(sizes[:chunk]), size) for chunk, size in enumerate(sizes)]
+
+
+def blend(pieces, width):
+    block = lax.broadcasted_iota(jnp.int32, pieces[0].shape, pieces[0].ndim - 1)
+    value = pieces[0]
+    for index, piece in enumerate(pieces[1:], 1):
+        value = jnp.where(block >= index * width, piece, value)
+    return value
+
+
+def turn(values, shift):
+    lanes = values.shape[-1]
+    return pltpu.roll(values, shift % lanes, values.ndim - 1) if shift % lanes else values
 
 
 def fused_kernel(
     width_gx, width_col, field_hbm, core_hbm, in_hbm, out_hbm, x_hbm, y_hbm, z_hbm, reach_hbm,
     x_pick_hbm, in_pick_hbm, z_pick_hbm, out_pick_hbm, y_pick_hbm, same_hbm, y_table_hbm,
-    z_table_hbm, fore_hbm, back_hbm, z_back_hbm, y_back_hbm, high_out, low_out, y_back_ref, field,
-    core_in, in_ref, out_ref, x_ref, y_ref, z_ref, reach_ref, x_pick_ref, in_pick_ref, z_pick_ref,
-    out_pick_ref, y_pick_ref, same_ref, y_table_ref, z_table_ref, fore_ref, back_ref, z_back_ref,
-    y_high, y_low, values_ref, spec, arrived, cores, cores_in, factor, factors, kept_ref, rank_ref,
-    high_ref, low_ref, plane_ref, result, returned, partial_ref, field_sems, load_sems, sends, recvs,
-    core_sends, core_recvs, factor_sends, factor_recvs, back_sends, back_recvs,
+    z_table_hbm, fore_hbm, back_hbm, y_back_hbm, *refs,
 ):
+    chunks = len(SHARES)
+    z_back_hbm, refs = refs[:chunks], refs[chunks:]
+    high_out, low_out, y_back_ref, *refs = refs
+    field, core_in, in_ref, out_ref, x_ref, y_ref, z_ref, reach_ref, *refs = refs
+    x_pick_ref, in_pick_ref, z_pick_ref, out_pick_ref, y_pick_ref, same_ref, *refs = refs
+    y_table_ref, z_table_ref, fore_ref, back_ref, *refs = refs
+    z_back_ref, refs = refs[:chunks], refs[chunks:]
+    spec, refs = refs[:chunks], refs[chunks:]
+    arrived, refs = refs[:chunks], refs[chunks:]
+    result, refs = refs[:chunks], refs[chunks:]
+    returned, refs = refs[:chunks], refs[chunks:]
+    y_high, y_low, values_ref, cores, cores_in, factor, factors, kept_ref, rank_ref, *refs = refs
+    plane_ref, partial_ref, field_sems, load_sems, sends, recvs, *refs = refs
+    core_sends, core_recvs, factor_sends, factor_recvs, back_sends, back_recvs = refs
     count = width_gx * width_col
     my_gx, my_col = lax.axis_index("gx"), lax.axis_index("col")
     me = my_gx * width_col + my_col
     channels, planes, _, grid_z = field.shape
-    _, modes_y, group, lanes = spec.shape
+    _, modes_y, lanes = values_ref.shape
     modes_x, modes_z = x_ref.shape[1], z_ref.shape[1]
+    lead = 2 * planes
     barrier = pltpu.get_barrier_semaphore()
     gx_steps = sorted(range(width_gx), key=lambda step: min(step, width_gx - step))
+    near = gx_steps[: width_gx // 2]
     col_steps = range(width_col)
 
     def slab_at(step):
@@ -231,34 +264,43 @@
                     device_id_type=MESH,
                 )
 
+    burst = channels // field_sems.shape[0]
+
     def fetch(channel):
         return pltpu.make_async_copy(
-            field_hbm.at[channel], field.at[channel], field_sems.at[channel]
+            field_hbm.at[channel], field.at[channel], field_sems.at[lax.div(channel, burst)]
         )
 
-    sources = [
-        y_table_hbm, z_table_hbm, core_hbm, y_hbm, y_pick_hbm, same_hbm, in_hbm, out_hbm,
-        in_pick_hbm, out_pick_hbm, x_hbm, z_hbm, reach_hbm, x_pick_hbm, z_pick_hbm, fore_hbm,
-        back_hbm, z_back_hbm, y_back_hbm,
-    ]
-    targets = [
-        y_table_ref, z_table_ref, core_in, y_ref, y_pick_ref, same_ref, in_ref, out_ref,
-        in_pick_ref, out_pick_ref, x_ref, z_ref, reach_ref, x_pick_ref, z_pick_ref, fore_ref,
-        back_ref, z_back_ref, y_back_ref,
+    stages = [
+        [(y_table_hbm, y_table_ref)],
+        [(z_table_hbm, z_table_ref)],
+        [(in_hbm, in_ref), (out_hbm, out_ref), (y_hbm, y_ref), (y_pick_hbm, y_pick_ref),
+         (same_hbm, same_ref)],
+        [(core_hbm, core_in)],
+        [(in_pick_hbm, in_pick_ref), (out_pick_hbm, out_pick_ref), (x_hbm, x_ref), (z_hbm, z_ref),
+         (reach_hbm, reach_ref), (x_pick_hbm, x_pick_ref), (z_pick_hbm, z_pick_ref),
+         (fore_hbm, fore_ref), (back_hbm, back_ref)],
+        [(y_back_hbm, y_back_ref), *zip(z_back_hbm, z_back_ref)],
     ]
     loads = [
-        pltpu.make_async_copy(source, target, load_sems.at[index])
-        for index, (source, target) in enumerate(zip(sources, targets))
+        [pltpu.make_async_copy(source, target, load_sems.at[stage]) for source, target in copies]
+        for stage, copies in enumerate(stages)
     ]
-    loads[0].start()
+
+    def await_loads(stage):
+        for load in loads[stage]:
+            load.wait()
+
+    loads[0][0].start()
 
     def begin(channel, carry):
         fetch(channel).start()
         return carry
 
     lax.fori_loop(0, channels, begin, 0)
-    for load in loads[1:]:
-        load.start()
+    for stage in loads[1:]:
+        for load in stage:
+            load.start()
 
     def remote(source, target, send_sem, recv_sem, device):
         return pltpu.make_async_remote_copy(
@@ -266,42 +308,59 @@
             device_id=device, device_id_type=MESH,
         )
 
-    loads[0].wait()
+    await_loads(0)
     half = 2 * modes_y
-    pair = 2
-    for part in range(HALVES):
+    batch = channels // 2
+    for part in range(2):
 
         def transform(step, carry, part=part):
-            for offset in range(pair):
-                local = step * pair + offset
-                channel = part * group + local
-                fetch(channel).wait()
+            first = part * batch + step * burst
+            pltpu.make_async_copy(
+                field_hbm.at[pl.ds(first, burst)], field.at[pl.ds(first, burst)],
+                field_sems.at[lax.div(first, burst)],
+            ).wait()
+            for offset in range(burst):
+                local = step * burst + offset
+                channel = first + offset
                 parts = []
-                for plane in range(planes):
-                    both = dot(y_table_ref[...], field[channel, plane])
+                for plane in range(0, planes, 2):
+                    two = jnp.concatenate([field[channel, plane], field[channel, plane + 1]], 1)
+                    both = dot(y_table_ref[...], two)
                     y_values = both[:half] + both[half:]
-                    parts += [y_values[:modes_y], y_values[modes_y:]]
+                    for at in (0, grid_z):
+                        parts += [
+                            y_values[:modes_y, at : at + grid_z],
+                            y_values[modes_y:, at : at + grid_z],
+                        ]
                 high, low = split(jnp.concatenate(parts, 1))
                 rows = pl.ds(pl.multiple_of(local * modes_y, modes_y), modes_y)
                 y_high[rows] = high
                 y_low[rows] = low
             return carry
 
-        lax.fori_loop(0, group // pair, transform, 0)
+        lax.fori_loop(0, batch // burst, transform, 0)
         if part == 0:
-            loads[1].wait()
+            await_loads(1)
         both = dot(y_high[...], z_table_ref[...])
         value = both[:, :lanes] + both[:, lanes:] + dot(y_low[...], z_table_ref[:, :lanes])
-        values_ref[part] = jnp.swapaxes(value.reshape(group, modes_y, lanes), 0, 1)
-
-    spot = lax.broadcasted_iota(jnp.int32, (modes_y, group, lanes), 2)
-    first, second = values_ref[0], values_ref[1]
-    middle = lanes // HALVES
-    spec[0] = jnp.where(spot < middle, first, pltpu.roll(second, middle, 2))
-    spec[1] = jnp.where(spot < middle, pltpu.roll(first, middle, 2), second)
-
-    for load in loads[2:10]:
-        load.wait()
+        values_ref[part * batch : (part + 1) * batch] = value.reshape(batch, modes_y, lanes)
+
+    sizes = []
+    for first, modes in mode_chunks(modes_z):
+        width = modes * lead
+        groups = lanes // width
+        sizes.append((first, modes, width, groups, channels // groups))
+
+    def pack(chunk):
+        first, _, width, groups, rows = sizes[chunk]
+        pieces = [
+            turn(values_ref[g * rows : (g + 1) * rows], g * width - first * lead)
+            for g in range(groups)
+        ]
+        spec[chunk][...] = jnp.swapaxes(blend(pieces, width), 0, 1)
+
+    pack(0)
+    await_loads(2)
     rank_out = in_ref.shape[1]
     factor[...] = jnp.concatenate(
         [in_ref[...], out_ref[...], jnp.zeros((channels, lanes - 2 * rank_out), F32)], 1
@@ -311,71 +370,72 @@
     spot = lax.broadcasted_iota(jnp.int32, row.shape, 1)
     rank_x = x_ref.shape[0]
     wanted = my_gx * width_col + lax.rem(lax.div(row, rank_x), width_col)
-    y_high_rows, y_low_rows = split(
-        spread(jnp.where(spot == wanted, 1.0, 0.0), y_wide, 1) * same_ref[...]
-    )
-    y_stack = jnp.concatenate([y_high_rows, y_low_rows], 0)
-    core_rows = y_wide.shape[1]
-    out_rows = same_ref.shape[0]
+    y_rows = spread(jnp.where(spot == wanted, 1.0, 0.0), y_wide, 1) * same_ref[...]
+    y_stack = jnp.concatenate(split(y_rows), 0)
+    out_rows, core_rows = y_rows.shape
     rank_z = lanes // rank_out
     spot_rows = width_col * rank_x
 
-    def contract(step, carry):
-        rows = pl.ds(pl.multiple_of(step * core_rows, core_rows), core_rows)
-        high, low = split(core_in[rows])
-        both = dot(y_stack, high)
-        value = both[:out_rows] + both[out_rows:] + dot(y_high_rows, low)
-        wide = jnp.concatenate(
-            [value[e * spot_rows : (e + 1) * spot_rows] for e in range(rank_z)], 1
-        )
-        place = pl.ds(pl.multiple_of(step * rank_x, rank_x), rank_x)
-        for target in range(width_col):
-            cores[target, place] = wide[target * rank_x : (target + 1) * rank_x]
-        return carry
-
-    lax.fori_loop(0, core_in.shape[0] // core_rows, contract, 0)
-
     pl.semaphore_wait(barrier, count - 1)
 
     def factor_copy(writer, device):
         return remote(
-            factor, factors.at[writer], factor_sends.at[0], factor_recvs.at[writer], device
+            factor, factors.at[writer], factor_sends.at[0], factor_recvs.at[0], device
         )
 
     def core_copy(peer, writer, device):
         return remote(
-            cores.at[peer], cores_in.at[writer], core_sends.at[0], core_recvs.at[writer], device
+            cores.at[peer], cores_in.at[writer], core_sends.at[0], core_recvs.at[0], device
         )
 
-    def send_half(part, source, target, send_sems, recv_sems):
+    def near_side(gx_step):
+        return 0 if (width_gx - gx_step) % width_gx in near else 1
+
+    def own_side(gx_step):
+        return lax.div(my_gx, width_gx // 2)
+
+    def send_chunk(chunk, source, target, send_sems, recv_sems, side_of):
         for gx_step in gx_steps:
             slab = slab_at(gx_step)
             for col_step in col_steps:
                 if gx_step or col_step:
                     column = col_at(col_step)
                     remote(
-                        source.at[part, slab * width_col + column], target.at[part, me],
-                        send_sems.at[part], recv_sems.at[part, my_gx], (slab, column),
+                        source[chunk].at[slab * width_col + column], target[chunk].at[me],
+                        send_sems.at[chunk], recv_sems.at[chunk, side_of(gx_step)], (slab, column),
                     ).start()
 
-    def receive(part, target, recv_sems, slab, messages):
-        block = target.at[part, pl.ds(0, messages)]
-        remote(block, block, recv_sems.at[part, slab], recv_sems.at[part, slab], (my_gx, my_col)
-               ).wait_recv()
-
+    def receive(chunk, target, recv_sem, messages):
+        block = target[chunk].at[pl.ds(0, messages)]
+        remote(block, block, recv_sem, recv_sem, (my_gx, my_col)).wait_recv()
+
+    send_chunk(0, spec, arrived, sends, recvs, near_side)
     for step in range(1, width_col):
         factor_copy(my_col, (my_gx, col_at(step))).start()
-    send_half(0, spec, arrived, sends, recvs)
+    await_loads(3)
+    for step in range(0, core_in.shape[0] // core_rows, rank_z):
+        tall = [core_in[(step + e) * core_rows : (step + e + 1) * core_rows] for e in range(rank_z)]
+        high, low = split(jnp.concatenate(tall, 1))
+        value = dot(y_stack, jnp.concatenate([high, low], 1))
+        value = value[:out_rows] + value[out_rows:]
+        value = value[:, :lanes] + value[:, lanes:]
+        for offset in range(rank_z):
+            pieces = [
+                turn(value[e * spot_rows : (e + 1) * spot_rows], (e - offset) * rank_out)
+                for e in range(rank_z)
+            ]
+            wide = blend(pieces, rank_out)
+            first = (step + offset) * rank_x
+            for target in range(width_col):
+                rows = wide[target * rank_x : (target + 1) * rank_x]
+                cores[target, first : first + rank_x] = rows
+
     for step in range(1, width_col):
         core_copy(col_at(step), my_col, (my_gx, col_at(step))).start()
-    send_half(1, spec, arrived, sends, recvs)
-
-    for part in range(HALVES):
-        arrived[part, me] = spec[part, me]
-    cores_in[my_col] = cores[my_col]
-    factors[my_col] = factor[...]
-    for load in loads[10:17]:
-        load.wait()
+    pack(1)
+    send_chunk(1, spec, arrived, sends, recvs, near_side)
+
+    await_loads(4)
     x_wide = spread(x_ref[...], x_pick_ref[...], 0)
     z_rows = spread(z_ref[...], z_pick_ref[...], 0)
     spot = lax.broadcasted_iota(jnp.int32, reach_ref.shape, 1)
@@ -385,131 +445,166 @@
     slot = jnp.where(slot < modes_x // 2, slot, modes_x - slot).astype(F32)
     for l in range(modes_z):
         kept_ref[l] = jnp.where(slot < reach[l : l + 1], x_wide, 0.0)
-
-    for step in range(1, width_col):
-        factor_copy(col_at(step), (my_gx, my_col)).wait_recv()
-    in_stack, out_parts = [], []
-    for part in range(HALVES):
-        rows = factors[:, part * group : (part + 1) * group].reshape(width_col * group, lanes)
-        in_high, in_low = split(spread(rows[:, :rank_out], in_pick_ref[...], 1))
-        in_stack += [in_high, in_low, in_high, in_low]
-        out_parts.append(spread(rows[:, rank_out : 2 * rank_out], out_pick_ref[...], 1))
-    in_stack = jnp.concatenate(in_stack, 0)
-    out_high, out_low = split(jnp.concatenate(out_parts, 0))
-    out_stack = jnp.concatenate([out_high, out_low], 0)
-    rows_out = out_high.shape[0]
-
-    lead = 2 * planes
-    modes_half = modes_z // HALVES
+    for chunk in range(2, chunks):
+        pack(chunk)
+        send_chunk(chunk, spec, arrived, sends, recvs, near_side)
+    for chunk in range(chunks):
+        arrived[chunk][me] = spec[chunk][me]
+    cores_in[my_col] = cores[my_col]
+    factors[my_col] = factor[...]
+
+    others = factors.at[pl.ds(0, width_col - 1)]
+    remote(others, others, factor_recvs.at[0], factor_recvs.at[0], (my_gx, my_col)).wait_recv()
+    rows = factors[...].reshape(width_col * channels, lanes)
+    in_rows = spread(rows[:, :rank_out], in_pick_ref[...], 1)
+    out_all = spread(rows[:, rank_out : 2 * rank_out], out_pick_ref[...], 1)
+
+    def regroup(values, groups):
+        values = values.reshape(width_col, groups, channels // groups, -1)
+        return [values[:, g].reshape(width_col * channels // groups, -1) for g in range(groups)]
+
+    in_stacks, out_stacks = {}, {}
+    for groups in sorted({size[3] for size in sizes}):
+        stack = []
+        for in_group in regroup(in_rows, groups):
+            in_high, in_low = split(in_group)
+            stack += [in_high, in_low, in_high, in_low]
+        in_stacks[groups] = jnp.concatenate(stack, 0)
+        out_stacks[groups] = split(jnp.concatenate(regroup(out_all, groups), 0))
+    rows_out = out_all.shape[0]
+
     both_modes = 2 * modes_x
     ranks = x_wide.shape[1]
     last = (((1,), (1,)), ((), ()))
 
-    def gather_ranks(part):
-        for gx_step in gx_steps:
-            slab = slab_at(gx_step)
-            receive(part, arrived, recvs, slab, width_col if gx_step else width_col - 1)
-            block = arrived[part, pl.ds(slab * width_col, width_col)]
-            block = block.reshape(width_col * group, lanes)
-            high = block.astype(BF16).astype(F32)
-            low = block - high
-            stacked = jnp.concatenate([high, high, low, low], 0).T.astype(BF16)
-            wide = jnp.concatenate([stacked[:middle], stacked[middle:]], 1)
-            value = dot(wide, in_stack).reshape(modes_half, lead, ranks)
-            rank_ref[:, pl.ds(pl.multiple_of(slab * lead, lead), lead)] = value
-
-    def mix(part, core_high, core_both):
-        for l in range(modes_half):
+    def gather_ranks(chunk):
+        _, modes, width, groups, rows = sizes[chunk]
+        copies = lanes // (4 * width_col * rows)
+        if chunk:
+            receive(chunk, arrived, recvs.at[chunk, 0], count // 2 - 1)
+            receive(chunk, arrived, recvs.at[chunk, 1], count // 2)
+            turns = [gx_steps]
+        else:
+            turns = [near, gx_steps[width_gx // 2 :]]
+        for side, steps in enumerate(turns):
+            if not chunk:
+                receive(chunk, arrived, recvs.at[chunk, side], count // 2 - 1 + side)
+            for gx_step in steps:
+                slab = slab_at(gx_step)
+                block = arrived[chunk][pl.ds(slab * width_col, width_col)]
+                block = block.reshape(width_col * rows, lanes)
+                stacked = []
+                for copy in range(copies):
+                    high, low = split(turn(block, -copy * width))
+                    stacked += [high, high, low, low]
+                stacked = jnp.concatenate(stacked, 0).T
+                wide = [
+                    stacked[g * width : (g + 1) * width] for g in range(0, groups, copies)
+                ]
+                value = dot(jnp.concatenate(wide, 1), in_stacks[groups])
+                value = value.reshape(modes, lead, ranks)
+                rank_ref[:modes, pl.ds(pl.multiple_of(slab * lead, lead), lead)] = value
+
+    def mix(chunk, core_high, core_low):
+        first, modes = sizes[chunk][:2]
+        parts = []
+        for l in range(modes):
             high, low = split(rank_ref[l])
             value = dot(fore_ref[...], jnp.concatenate([high, low, high], 0))
-            kept = kept_ref[part * modes_half + l]
-            value = value * jnp.concatenate([kept] * 4, 0)
-            value = jnp.concatenate([value[:both_modes], value[both_modes:]], 1)
-            rows = slice(l * both_modes, (l + 1) * both_modes)
-            high_ref[rows], low_ref[rows] = split(value)
-        both = dot(high_ref[...], core_both)
-        mixed = both[:, :lanes] + both[:, lanes:] + dot(low_ref[...], core_high)
-        for l in range(modes_half):
-            at = part * modes_half + l
-            value = mixed[l * both_modes : (l + 1) * both_modes] * z_rows[at : at + 1]
-            high, low = split(value)
+            parts.append(split(value * jnp.concatenate([kept_ref[first + l]] * 2, 0)))
+        mixed = []
+        for start in (0, modes // 2):
+            high, low = (
+                jnp.concatenate(rows, 0) for rows in zip(*parts[start : start + modes // 2])
+            )
+            mixed.append(dot(high, core_high) + dot(low, core_high) + dot(high, core_low))
+        for l in range(modes):
+            both = mixed[l // (modes // 2)]
+            at = l % (modes // 2) * both_modes
+            real, imag = both[at : at + modes_x], both[at + modes_x : at + both_modes]
+            value = jnp.concatenate(
+                [real[:, :lanes] - imag[:, lanes:], real[:, lanes:] + imag[:, :lanes]], 0
+            )
+            high, low = split(value * z_rows[first + l : first + l + 1])
             value = dot(back_ref[...], jnp.concatenate([high, low, high], 0))
             plane_ref[:, l] = value.reshape(width_gx, lead, lanes)
 
-    def expand(part):
-        spot = lax.broadcasted_iota(jnp.int32, (rows_out // HALVES, lanes), 1)
-        for slab in range(0, width_gx, HALVES):
-            rows = plane_ref[slab : slab + HALVES].reshape(lanes, lanes)
-            high, low = split(rows)
+    def expand(chunk):
+        _, modes, width, groups, rows = sizes[chunk]
+        out_high, out_low = out_stacks[groups]
+        out_stack = jnp.concatenate([out_high, out_low], 0)
+        group_rows = width_col * rows
+        for slab in range(0, width_gx, groups):
+            high, low = split(plane_ref[slab : slab + groups, :modes].reshape(lanes, lanes))
             both = lax.dot_general(out_stack, high, last, preferred_element_type=F32)
             value = both[:rows_out] + both[rows_out:]
             value = value + lax.dot_general(out_high, low, last, preferred_element_type=F32)
-            first, second = value[: rows_out // HALVES], value[rows_out // HALVES :]
-            pieces = (
-                jnp.where(spot < middle, first, pltpu.roll(second, middle, 1)),
-                jnp.where(spot < middle, pltpu.roll(first, middle, 1), second),
-            )
-            for offset, piece in enumerate(pieces):
+            for offset in range(groups):
+                pieces = [
+                    turn(value[g * group_rows : (g + 1) * group_rows], (g - offset) * width)
+                    for g in range(groups)
+                ]
                 at = (slab + offset) * width_col
-                result[part, at : at + width_col] = piece.reshape(width_col, group, lanes)
-
-    for part in range(HALVES):
-        gather_ranks(part)
-        if part == 0:
-            for step in range(1, width_col):
-                core_copy(my_col, col_at(step), (my_gx, my_col)).wait_recv()
+                piece = blend(pieces, width).reshape(width_col, rows, lanes)
+                result[chunk][at : at + width_col] = piece
+
+    for chunk in range(chunks):
+        gather_ranks(chunk)
+        if chunk == 0:
+            others = cores_in.at[pl.ds(0, width_col - 1)]
+            remote(others, others, core_recvs.at[0], core_recvs.at[0], (my_gx, my_col)).wait_recv()
             half_rows = cores.shape[1] // 2
             core = [cores_in[:, first : first + half_rows] for first in (0, half_rows)]
-            core = jnp.concatenate([rows.reshape(ranks, lanes) for rows in core], 0)
+            core = jnp.concatenate([rows.reshape(ranks, lanes) for rows in core], 1)
             core_high, core_low = split(core)
-            core_both = jnp.concatenate([core_high, core_low], 1)
-        mix(part, core_high, core_both)
-        expand(part)
-        send_half(part, result, returned, back_sends, back_recvs)
-        returned[part, me] = result[part, me]
-
-    loads[17].wait()
+        mix(chunk, core_high, core_low)
+        expand(chunk)
+        send_chunk(chunk, result, returned, back_sends, back_recvs, own_side)
+        returned[chunk][me] = result[chunk][me]
+
+    await_loads(5)
     ky_half = modes_y // 2
     gx_half = width_gx // 2
     my_half = lax.div(my_gx, gx_half)
-    spot = lax.broadcasted_iota(jnp.int32, (group * ky_half, lanes), 1)
     wide = 2 * grid_z
-    for part in range(HALVES):
-        for turn in range(2):
-            side = lax.rem(my_half + turn, 2)
-            for step in range(gx_half):
-                slab = side * gx_half + lax.rem(my_gx + step, gx_half)
-                full = turn > 0 or step > 0
-                receive(part, returned, back_recvs, slab, width_col if full else width_col - 1)
-            block = returned[part, pl.ds(side * ky_half, ky_half)]
-            block = jnp.swapaxes(block, 0, 1).reshape(group * ky_half, lanes)
+    for chunk in range(chunks):
+        _, _, width, groups, rows = sizes[chunk]
+        for side_step in range(2):
+            side = lax.rem(my_half + side_step, 2)
+            receive(chunk, returned, back_recvs.at[chunk, side], count // 2 - 1 + side_step)
+            block = returned[chunk][pl.ds(side * ky_half, ky_half)]
+            block = jnp.swapaxes(block, 0, 1).reshape(rows * ky_half, lanes)
             high = block.astype(BF16).astype(F32)
             low = block - high
-            high_turned, low_turned = pltpu.roll(high, middle, 1), pltpu.roll(low, middle, 1)
-            one = [jnp.where(spot < middle, high, low_turned), high[:, :middle]]
-            two = [jnp.where(spot < middle, high_turned, low), high_turned[:, :middle]]
-            stacked = jnp.concatenate(
-                [jnp.concatenate(one, 1), jnp.concatenate(two, 1)], 0
-            ).astype(BF16)
-            rows = pl.ds(pl.multiple_of(side * ky_half, ky_half), ky_half)
+            stacked = []
+            for g in range(groups):
+                pieces = [
+                    turn(value, (spot - g) * width) for spot, value in enumerate((high, low, high))
+                ]
+                tiles = [
+                    blend(pieces[tile : tile + groups], width) for tile in range(0, 3, groups)
+                ]
+                stacked.append(jnp.concatenate(tiles, 1)[:, : 3 * width])
+            stacked = jnp.concatenate(stacked, 0).astype(BF16)
+            spots = pl.ds(pl.multiple_of(side * ky_half, ky_half), ky_half)
             for plane in range(planes):
                 at = slice(plane * wide, (plane + 1) * wide)
-                value = dot(stacked, z_back_ref[part, :, at]).reshape(channels, ky_half, wide)
-                if part + 1 < HALVES:
-                    partial_ref[:, rows, at] = value
+                value = dot(stacked, z_back_ref[chunk][:, at]).reshape(channels, ky_half, wide)
+                if chunk > 0:
+                    value = value + partial_ref[:, spots, at]
+                if chunk + 1 < chunks:
+                    partial_ref[:, spots, at] = value
                 else:
-                    value = value + partial_ref[:, rows, at]
-                    high_out[:, rows, at], low_out[:, rows, at] = split(value)
-
-    loads[18].wait()
+                    high_out[:, spots, at], low_out[:, spots, at] = split(value)
+
     for source, send_sem in ((factors, factor_sends.at[0]), (cores, core_sends.at[0])):
         block = source.at[pl.ds(0, width_col - 1)]
         remote(block, block, send_sem, send_sem, (my_gx, my_col)).wait_send()
-    for part in range(HALVES):
+    for chunk in range(chunks):
         for target, send_sems in ((spec, sends), (result, back_sends)):
-            block = target.at[part, pl.ds(0, count - 1)]
-            remote(block, block, send_sems.at[part], send_sems.at[part], (my_gx, my_col)
-                   ).wait_send()
+            block = target[chunk].at[pl.ds(0, count - 1)]
+            sem = send_sems.at[chunk]
+            remote(block, block, sem, sem, (my_gx, my_col)).wait_send()
 
 
 def fused(
@@ -522,19 +617,24 @@
     modes_z, rank_z = z_factor.shape
     rank_in, rank_out = in_factor.shape[1], out_factor.shape[1]
     y_table, z_table = forward_tables(grid_y, grid_z, modes_y, modes_z, planes)
-    y_back, z_back = inverse_tables(grid_y, grid_z, modes_y, modes_z, planes, HALVES)
+    y_back, z_back = inverse_tables(grid_y, grid_z, modes_y, modes_z, planes)
     fore, back = x_tables(planes * width_gx, modes_x)
     picks = selectors(width_col, rank_in, rank_x, rank_y, rank_z, rank_out)
     count = width_gx * width_col
     lanes, wide = planes * 2 * modes_z, planes * 2 * grid_z
     ranks = rank_in * rank_x
-    group = channels // HALVES
     dma = pltpu.SemaphoreType.DMA
-    tables = [jnp.asarray(t) for t in picks + [y_table, z_table, fore, back, z_back, y_back]]
+    chunks = mode_chunks(modes_z)
+    most = max(modes for _, modes in chunks)
+    exchange = [
+        pltpu.VMEM((count, channels * modes // modes_z, lanes), F32) for _, modes in chunks
+    ]
+    tables = [jnp.asarray(t) for t in picks + [y_table, z_table, fore, back, y_back] + z_back]
     small = [in_factor, out_factor, x_factor.T, y_factor.T, z_factor.T, kx_reach.T]
     operands = [grid_field, core] + small + tables
+    keep = len(operands) - len(chunks) - 1
+    loaded = operands[:keep] + operands[keep + 1 :]
     core_rows = 2 * rank_in // width_col * rank_x
-    exchange = (HALVES, count, group, lanes)
     return pl.pallas_call(
         functools.partial(fused_kernel, width_gx, width_col),
         out_shape=[
@@ -544,35 +644,30 @@
         ],
         in_specs=[pl.BlockSpec(memory_space=pltpu.HBM)] * len(operands),
         out_specs=[VMEM] * 3,
-        scratch_shapes=[pltpu.VMEM(a.shape, a.dtype) for a in operands[:-1]]
+        scratch_shapes=[pltpu.VMEM(a.shape, a.dtype) for a in loaded]
+        + exchange * 4
         + [
-            pltpu.VMEM((group * modes_y, wide), BF16),
-            pltpu.VMEM((group * modes_y, wide), BF16),
-            pltpu.VMEM((HALVES, modes_y, group, lanes), F32),
-            pltpu.VMEM(exchange, F32),
-            pltpu.VMEM(exchange, F32),
+            pltpu.VMEM((channels // 2 * modes_y, wide), BF16),
+            pltpu.VMEM((channels // 2 * modes_y, wide), BF16),
+            pltpu.VMEM((channels, modes_y, lanes), F32),
             pltpu.VMEM((width_col, core_rows, lanes), F32),
             pltpu.VMEM((width_col, core_rows, lanes), F32),
             pltpu.VMEM((channels, lanes), F32),
             pltpu.VMEM((width_col, channels, lanes), F32),
             pltpu.VMEM((modes_z, modes_x, ranks), F32),
-            pltpu.VMEM((modes_z // HALVES, 2 * planes * width_gx, ranks), F32),
-            pltpu.VMEM((modes_z // HALVES * 2 * modes_x, 2 * ranks), BF16),
-            pltpu.VMEM((modes_z // HALVES * 2 * modes_x, 2 * ranks), BF16),
-            pltpu.VMEM((width_gx, modes_z // HALVES, 2 * planes, lanes), F32),
-            pltpu.VMEM(exchange, F32),
-            pltpu.VMEM(exchange, F32),
+            pltpu.VMEM((most, 2 * planes * width_gx, ranks), F32),
+            pltpu.VMEM((width_gx, most, 2 * planes, lanes), F32),
             pltpu.VMEM((channels, modes_y, wide), F32),
-            dma((channels,)),
-            dma((len(operands) - 1,)),
-            dma((HALVES,)),
-            dma((HALVES, width_gx)),
+            dma((4,)),
+            dma((6,)),
+            dma((len(chunks),)),
+            dma((len(chunks), 2)),
             dma((1,)),
-            dma((width_col,)),
             dma((1,)),
-            dma((width_col,)),
-            dma((HALVES,)),
-            dma((HALVES, width_gx)),
+            dma((1,)),
+            dma((1,)),
+            dma((len(chunks),)),
+            dma((len(chunks), 2)),
         ],
         compiler_params=pltpu.CompilerParams(
             collective_id=0, has_side_effects=True, vmem_limit_bytes=VMEM_BYTES
@@ -582,6 +677,7 @@
 
 VMEM_BYTES = 40 * 2**20
 INVERSE_BYTES = 16 * 2**20
+INVERSE_UNROLL = 8
 
 
 def inverse_kernel(high_ref, low_ref, y_ref, out_hbm, out, sems):
@@ -607,7 +703,7 @@
         leave(channel).start()
         return carry
 
-    lax.fori_loop(0, channels, transform, 0)
+    lax.fori_loop(0, channels, transform, 0, unroll=INVERSE_UNROLL)
 
     def finish(channel, carry):
         leave(channel).wait()

time: 36 us -> 27.8 us (0.77)
  Pallas kernels: 35.8 us -> 27.7 us
    pallas_call x1, Pallas kernels: 31.4 us -> 25.3 us  [fused(): pl.pallas_call(functools.partial(fused_kernel, width_gx, width_col), out_...]
    pallas_call x1, Pallas kernels: 4.42 us -> 2.38 us  [inverse(): pl.pallas_call(inverse_kernel, in_specs=[VMEM] * 3, out_specs=pl.BlockSpe...]
where the time goes in v2:
time: 27.8 us; the launch traced here: 27.7 us
  Pallas kernels  27.7 us (100%)
    pallas_call x1, Pallas kernels, fused(): pl.pallas_call(functools.partial(fused_kernel, width_gx, width_col), out_...  25.3 us
    pallas_call x1, Pallas kernels, inverse(): pl.pallas_call(inverse_kernel, in_specs=[VMEM] * 3, out_specs=pl.BlockSpe...  2.38 us

profile of v2, /device:TPU:0, one launch (start us, length us, event | category | flops | bytes accessed | tf_op | source)
XLA Modules:
  0.0 27.7 jit_solution(11959026566688027899)
XLA Ops:
  0.0 25.3 %shard_map.199 = (bf16[16,32,1024]{2,1,0:T(8,128)(2,1)S(1)}, bf16[16,32,1024]{2,1,0:T(8,128)(2,1)S(1)}, bf16[256,192]{1,0:T(8,128)(2,1)S(1)}) custom-call(bf16[16,4,256,128]{3,2,1,0:T(8,128)(2,1)} %field_hbm.1, f32[4096,32]{1,0:T(8,128)} %bitcast.7, f32[16,32]{1,0:T(8,128)} %in_hbm.1, f32[16,32]{1,0:T(8,128)} %out_hbm.1, f32[8,32]{1,0:T(8,128)} %bitcast.9, ...), custom_call_target="tpu_custom_call" | custom-call | tf_op jit(solution)/shard_map/pallas_call | solution.py:638
  25.3 2.4 %shard_map.200 = bf16[16,4,256,128]{3,2,1,0:T(8,128)(2,1)} custom-call(bf16[16,32,1024]{2,1,0:T(8,128)(2,1)S(1)} %get-tuple-element.8.high_ref, bf16[16,32,1024]{2,1,0:T(8,128)(2,1)S(1)} %get-tuple-element.9.low_ref, bf16[256,192]{1,0:T(8,128)(2,1)S(1)} %get-tuple-element.10.y_ref), custom_call_target="tpu_custom_call" | custom-call | tf_op jit(solution)/shard_map/pallas_call | solution.py:716

commit v3 on v2

--- a/solution.py
+++ b/solution.py
@@ -155,10 +155,13 @@
         table[:, plane, 0, plane, 1, :] = sin_z
         table[:, plane, 1, plane, 1, :] = cos_z
     high, low = split_np(table.reshape(modes_z, planes * 2, -1))
+    chunks = mode_chunks(modes_z)
     z_tables = []
-    for first, modes in mode_chunks(modes_z):
-        parts = [part[first : first + modes] for part in (high, high, low)]
-        z_tables.append(np.concatenate(parts, 0).reshape(3 * modes * planes * 2, -1))
+    for family in families(modes_z):
+        parts = []
+        for first, modes in [chunks[chunk] for chunk in family]:
+            parts += [part[first : first + modes] for part in (high, high, low)]
+        z_tables.append(np.concatenate(parts, 0).reshape(-1, high.shape[-1]))
     return y_table, z_tables
 
 
@@ -206,6 +209,15 @@
     return [(sum(sizes[:chunk]), size) for chunk, size in enumerate(sizes)]
 
 
+def families(modes_z):
+    groups = []
+    for chunk, (first, _) in enumerate(mode_chunks(modes_z)):
+        if 2 * first % modes_z == 0:
+            groups.append([])
+        groups[-1].append(chunk)
+    return groups
+
+
 def blend(pieces, width):
     block = lax.broadcasted_iota(jnp.int32, pieces[0].shape, pieces[0].ndim - 1)
     value = pieces[0]
@@ -225,12 +237,13 @@
     z_table_hbm, fore_hbm, back_hbm, y_back_hbm, *refs,
 ):
     chunks = len(SHARES)
-    z_back_hbm, refs = refs[:chunks], refs[chunks:]
+    parts = len(families(sum(SHARES)))
+    z_back_hbm, refs = refs[:parts], refs[parts:]
     high_out, low_out, y_back_ref, *refs = refs
     field, core_in, in_ref, out_ref, x_ref, y_ref, z_ref, reach_ref, *refs = refs
     x_pick_ref, in_pick_ref, z_pick_ref, out_pick_ref, y_pick_ref, same_ref, *refs = refs
     y_table_ref, z_table_ref, fore_ref, back_ref, *refs = refs
-    z_back_ref, refs = refs[:chunks], refs[chunks:]
+    z_back_ref, refs = refs[: len(z_back_hbm)], refs[len(z_back_hbm) :]
     spec, refs = refs[:chunks], refs[chunks:]
     arrived, refs = refs[:chunks], refs[chunks:]
     result, refs = refs[:chunks], refs[chunks:]
@@ -256,14 +269,6 @@
     def col_at(step):
         return lax.rem(my_col + step, width_col)
 
-    for gx_step in gx_steps:
-        for col_step in col_steps:
-            if gx_step or col_step:
-                pl.semaphore_signal(
-                    barrier, inc=1, device_id=(slab_at(gx_step), col_at(col_step)),
-                    device_id_type=MESH,
-                )
-
     burst = channels // field_sems.shape[0]
 
     def fetch(channel):
@@ -272,10 +277,9 @@
         )
 
     stages = [
+        [(y_hbm, y_ref), (y_pick_hbm, y_pick_ref), (same_hbm, same_ref)],
         [(y_table_hbm, y_table_ref)],
-        [(z_table_hbm, z_table_ref)],
-        [(in_hbm, in_ref), (out_hbm, out_ref), (y_hbm, y_ref), (y_pick_hbm, y_pick_ref),
-         (same_hbm, same_ref)],
+        [(z_table_hbm, z_table_ref), (in_hbm, in_ref), (out_hbm, out_ref)],
         [(core_hbm, core_in)],
         [(in_pick_hbm, in_pick_ref), (out_pick_hbm, out_pick_ref), (x_hbm, x_ref), (z_hbm, z_ref),
          (reach_hbm, reach_ref), (x_pick_hbm, x_pick_ref), (z_pick_hbm, z_pick_ref),
@@ -291,16 +295,23 @@
         for load in loads[stage]:
             load.wait()
 
-    loads[0][0].start()
-
-    def begin(channel, carry):
-        fetch(channel).start()
-        return carry
-
-    lax.fori_loop(0, channels, begin, 0)
-    for stage in loads[1:]:
-        for load in stage:
-            load.start()
+    def begin(first, after):
+        for channel in range(first, min(first + channels // 2, channels)):
+            fetch(channel).start()
+        for stage in after:
+            for load in loads[stage]:
+                load.start()
+
+    for load in loads[0] + loads[1]:
+        load.start()
+    begin(0, [])
+    for gx_step in gx_steps:
+        for col_step in col_steps:
+            if gx_step or col_step:
+                pl.semaphore_signal(
+                    barrier, inc=1, device_id=(slab_at(gx_step), col_at(col_step)),
+                    device_id_type=MESH,
+                )
 
     def remote(source, target, send_sem, recv_sem, device):
         return pltpu.make_async_remote_copy(
@@ -308,7 +319,9 @@
             device_id=device, device_id_type=MESH,
         )
 
-    await_loads(0)
+    begin(channels // 2, [2])
+    rank_out = in_ref.shape[1]
+    await_loads(1)
     half = 2 * modes_y
     batch = channels // 2
     for part in range(2):
@@ -340,7 +353,8 @@
 
         lax.fori_loop(0, batch // burst, transform, 0)
         if part == 0:
-            await_loads(1)
+            begin(channels, [3, 4, 5])
+            await_loads(2)
         both = dot(y_high[...], z_table_ref[...])
         value = both[:, :lanes] + both[:, lanes:] + dot(y_low[...], z_table_ref[:, :lanes])
         values_ref[part * batch : (part + 1) * batch] = value.reshape(batch, modes_y, lanes)
@@ -360,11 +374,46 @@
         spec[chunk][...] = jnp.swapaxes(blend(pieces, width), 0, 1)
 
     pack(0)
-    await_loads(2)
-    rank_out = in_ref.shape[1]
     factor[...] = jnp.concatenate(
         [in_ref[...], out_ref[...], jnp.zeros((channels, lanes - 2 * rank_out), F32)], 1
     )
+    pl.semaphore_wait(barrier, count - 1)
+
+    def factor_copy(writer, device):
+        return remote(
+            factor, factors.at[writer], factor_sends.at[0], factor_recvs.at[0], device
+        )
+
+    def core_copy(peer, writer, device):
+        return remote(
+            cores.at[peer], cores_in.at[writer], core_sends.at[0], core_recvs.at[0], device
+        )
+
+    def near_side(gx_step):
+        return 0 if (width_gx - gx_step) % width_gx in near else 1
+
+    def own_side(gx_step):
+        return lax.div(my_gx, width_gx // 2)
+
+    def send_chunk(chunk, source, target, send_sems, recv_sems, side_of):
+        for gx_step in gx_steps:
+            slab = slab_at(gx_step)
+            for col_step in col_steps:
+                if gx_step or col_step:
+                    column = col_at(col_step)
+                    remote(
+                        source[chunk].at[slab * width_col + column], target[chunk].at[me],
+                        send_sems.at[chunk], recv_sems.at[chunk, side_of(gx_step)], (slab, column),
+                    ).start()
+
+    def receive(chunk, target, recv_sem, messages):
+        block = target[chunk].at[pl.ds(0, messages)]
+        remote(block, block, recv_sem, recv_sem, (my_gx, my_col)).wait_recv()
+
+    send_chunk(0, spec, arrived, sends, recvs, near_side)
+    for step in range(1, width_col):
+        factor_copy(my_col, (my_gx, col_at(step))).start()
+    await_loads(0)
     y_wide = spread(y_ref[...], y_pick_ref[...], 0)
     row = lax.broadcasted_iota(jnp.int32, (same_ref.shape[0], y_wide.shape[0]), 0)
     spot = lax.broadcasted_iota(jnp.int32, row.shape, 1)
@@ -376,42 +425,6 @@
     rank_z = lanes // rank_out
     spot_rows = width_col * rank_x
 
-    pl.semaphore_wait(barrier, count - 1)
-
-    def factor_copy(writer, device):
-        return remote(
-            factor, factors.at[writer], factor_sends.at[0], factor_recvs.at[0], device
-        )
-
-    def core_copy(peer, writer, device):
-        return remote(
-            cores.at[peer], cores_in.at[writer], core_sends.at[0], core_recvs.at[0], device
-        )
-
-    def near_side(gx_step):
-        return 0 if (width_gx - gx_step) % width_gx in near else 1
-
-    def own_side(gx_step):
-        return lax.div(my_gx, width_gx // 2)
-
-    def send_chunk(chunk, source, target, send_sems, recv_sems, side_of):
-        for gx_step in gx_steps:
-            slab = slab_at(gx_step)
-            for col_step in col_steps:
-                if gx_step or col_step:
-                    column = col_at(col_step)
-                    remote(
-                        source[chunk].at[slab * width_col + column], target[chunk].at[me],
-                        send_sems.at[chunk], recv_sems.at[chunk, side_of(gx_step)], (slab, column),
-                    ).start()
-
-    def receive(chunk, target, recv_sem, messages):
-        block = target[chunk].at[pl.ds(0, messages)]
-        remote(block, block, recv_sem, recv_sem, (my_gx, my_col)).wait_recv()
-
-    send_chunk(0, spec, arrived, sends, recvs, near_side)
-    for step in range(1, width_col):
-        factor_copy(my_col, (my_gx, col_at(step))).start()
     await_loads(3)
     for step in range(0, core_in.shape[0] // core_rows, rank_z):
         tall = [core_in[(step + e) * core_rows : (step + e + 1) * core_rows] for e in range(rank_z)]
@@ -432,9 +445,9 @@
 
     for step in range(1, width_col):
         core_copy(col_at(step), my_col, (my_gx, col_at(step))).start()
+
     pack(1)
     send_chunk(1, spec, arrived, sends, recvs, near_side)
-
     await_loads(4)
     x_wide = spread(x_ref[...], x_pick_ref[...], 0)
     z_rows = spread(z_ref[...], z_pick_ref[...], 0)
@@ -567,32 +580,36 @@
     gx_half = width_gx // 2
     my_half = lax.div(my_gx, gx_half)
     wide = 2 * grid_z
-    for chunk in range(chunks):
-        _, _, width, groups, rows = sizes[chunk]
+    for turn_at, family in enumerate(families(modes_z)):
+        _, _, width, groups, rows = sizes[family[0]]
         for side_step in range(2):
             side = lax.rem(my_half + side_step, 2)
-            receive(chunk, returned, back_recvs.at[chunk, side], count // 2 - 1 + side_step)
-            block = returned[chunk][pl.ds(side * ky_half, ky_half)]
-            block = jnp.swapaxes(block, 0, 1).reshape(rows * ky_half, lanes)
-            high = block.astype(BF16).astype(F32)
-            low = block - high
+            sources = []
+            for chunk in family:
+                receive(chunk, returned, back_recvs.at[chunk, side], count // 2 - 1 + side_step)
+                block = returned[chunk][pl.ds(side * ky_half, ky_half)]
+                block = jnp.swapaxes(block, 0, 1).reshape(rows * ky_half, lanes)
+                high = block.astype(BF16).astype(F32)
+                sources += [high, block - high, high]
             stacked = []
             for g in range(groups):
                 pieces = [
-                    turn(value, (spot - g) * width) for spot, value in enumerate((high, low, high))
+                    turn(value, (spot - g) * width) for spot, value in enumerate(sources)
                 ]
                 tiles = [
-                    blend(pieces[tile : tile + groups], width) for tile in range(0, 3, groups)
+                    blend(pieces[tile : tile + groups], width)
+                    for tile in range(0, len(pieces), groups)
                 ]
-                stacked.append(jnp.concatenate(tiles, 1)[:, : 3 * width])
+                stacked.append(jnp.concatenate(tiles, 1)[:, : len(pieces) * width])
             stacked = jnp.concatenate(stacked, 0).astype(BF16)
             spots = pl.ds(pl.multiple_of(side * ky_half, ky_half), ky_half)
             for plane in range(planes):
                 at = slice(plane * wide, (plane + 1) * wide)
-                value = dot(stacked, z_back_ref[chunk][:, at]).reshape(channels, ky_half, wide)
-                if chunk > 0:
+                value = dot(stacked, z_back_ref[turn_at][:, at])
+                value = value.reshape(channels, ky_half, wide)
+                if turn_at > 0:
                     value = value + partial_ref[:, spots, at]
-                if chunk + 1 < chunks:
+                if turn_at + 1 < len(z_back_ref):
                     partial_ref[:, spots, at] = value
                 else:
                     high_out[:, spots, at], low_out[:, spots, at] = split(value)
@@ -632,7 +649,7 @@
     tables = [jnp.asarray(t) for t in picks + [y_table, z_table, fore, back, y_back] + z_back]
     small = [in_factor, out_factor, x_factor.T, y_factor.T, z_factor.T, kx_reach.T]
     operands = [grid_field, core] + small + tables
-    keep = len(operands) - len(chunks) - 1
+    keep = len(operands) - len(z_back) - 1
     loaded = operands[:keep] + operands[keep + 1 :]
     core_rows = 2 * rank_in // width_col * rank_x
     return pl.pallas_call(

time: 27.8 us -> 27.3 us (0.982)
  Pallas kernels: 27.7 us -> 27.1 us
    pallas_call x1, Pallas kernels: 25.3 us -> 24.8 us  [fused(): pl.pallas_call(functools.partial(fused_kernel, width_gx, width_col), out_...]
where the time goes in v3:
time: 27.3 us; the launch traced here: 27.1 us
  Pallas kernels  27.1 us (99%)
    pallas_call x1, Pallas kernels, fused(): pl.pallas_call(functools.partial(fused_kernel, width_gx, width_col), out_...  24.8 us
    pallas_call x1, Pallas kernels, inverse(): pl.pallas_call(inverse_kernel, in_specs=[VMEM] * 3, out_specs=pl.BlockSpe...  2.38 us

profile of v3, /device:TPU:0, one launch (start us, length us, event | category | flops | bytes accessed | tf_op | source)
XLA Modules:
  0.0 27.1 jit_solution(1467759273226279844)
XLA Ops:
  0.0 24.8 %shard_map.199 = (bf16[16,32,1024]{2,1,0:T(8,128)(2,1)S(1)}, bf16[16,32,1024]{2,1,0:T(8,128)(2,1)S(1)}, bf16[256,192]{1,0:T(8,128)(2,1)S(1)}) custom-call(bf16[16,4,256,128]{3,2,1,0:T(8,128)(2,1)} %field_hbm.1, f32[4096,32]{1,0:T(8,128)} %bitcast.7, f32[16,32]{1,0:T(8,128)} %in_hbm.1, f32[16,32]{1,0:T(8,128)} %out_hbm.1, f32[8,32]{1,0:T(8,128)} %bitcast.9, ...), custom_call_target="tpu_custom_call" | custom-call | tf_op jit(solution)/shard_map/pallas_call | solution.py:655
  24.8 2.4 %shard_map.200 = bf16[16,4,256,128]{3,2,1,0:T(8,128)(2,1)} custom-call(bf16[16,32,1024]{2,1,0:T(8,128)(2,1)S(1)} %get-tuple-element.8.high_ref, bf16[16,32,1024]{2,1,0:T(8,128)(2,1)S(1)} %get-tuple-element.9.low_ref, bf16[256,192]{1,0:T(8,128)(2,1)S(1)} %get-tuple-element.10.y_ref), custom_call_target="tpu_custom_call" | custom-call | tf_op jit(solution)/shard_map/pallas_call | solution.py:733
